TPU v7x, 32 devices: a whole 2x2x4 slice. The times are simulated.
32 devices in a mesh: row: 8 (over z, x), col: 4 (over y, core).
Axes of the slice: x: 2, y: 2, z: 4, core: 2. Of those that a mesh axis runs over, the one named last changes fastest.
Arguments:
- charges: float32 [32768], P(('row', 'col')), may hold values from -0.5 to 1.5
- structure_id: int32 [32768], P(('row', 'col')), may hold values from 0 to 255, as said below
- live_count: int32 [32], P(('row', 'col')), may hold values from 512 to 1024, as said below
- cell_index: int32 [3, 32768], P(None, ('row', 'col')), may hold values from 0 to 255, as said below
- fraction: float32 [3, 32768], P(None, ('row', 'col')), may hold values from 0 to 1
- influence: float32 [256, 64, 64], P('col', 'row'), may hold values from 0.1 to 10
Outputs:
- forces: float32 [3, 32768], P(None, ('row', 'col'))
- atom_energy: float32 [32768], P(('row', 'col'))
Inputs may be any that keep to these rules, and one draw needn't show every extreme that they name: `structure_id`: devices are numbered row-major over (row, col). Slots 0 to 7 of device d are live and belong to fragments d * 8 to d * 8 + 7, so every fragment has a live atom; every other slot names a fragment of its own device, of one of the four devices beside it along row or col (wrapping around), or of the device whose number is d plus half the number of devices (wrapping around). Device d's live atoms are its first live_count[d] slots; the count reaches 1024 on some device in every draw. `cell_index`: the atom slots of the device at (row r, col c) lie in its mesh block: first index from r * 8 to r * 8 + 7, second from c * 16 to c * 16 + 15; the third is anywhere.
All inputs are finite; a program needn't handle non-finite values.
Results may differ from a plain program's by a relative error of at most 0.000065.
Values sent between devices are 32-bit elements; how exact they have to be, the bound alone decides.
A program may use at most 64 MiB of HBM per device.

v0:
```python
import math

import functools

import jax
import jax.numpy as jnp
import numpy as np
from jax import lax
from jax.experimental import pallas as pl
from jax.experimental.pallas import tpu as pltpu
from jax.sharding import PartitionSpec as P

CX = 8
CY = 16
NZ = 256
S_DEV = 8


highest = lax.Precision.HIGHEST


def passed_along(block, axis, distance):
    devices = range(lax.axis_size(axis))
    route = [((i - distance) % len(devices), i) for i in devices]
    return lax.ppermute(block, axis, route)


def spline_weights(fraction):
    remain = 1.0 - fraction
    square = fraction * fraction
    cubic_term = square * fraction
    values = [
        remain * remain * remain / 6.0,
        (3.0 * cubic_term - 6.0 * square + 4.0) / 6.0,
        (-3.0 * cubic_term + 3.0 * square + 3.0 * fraction + 1.0) / 6.0,
        cubic_term / 6.0,
    ]
    slopes = [
        -0.5 * remain * remain,
        0.5 * (3.0 * square - 4.0 * fraction),
        0.5 * (-3.0 * square + 2.0 * fraction + 1.0),
        0.5 * square,
    ]
    return (values, slopes)


def place_weights(weights, local, width, period):
    columns = lax.broadcasted_iota(jnp.int32, (local.shape[0], width), 1)
    result = jnp.zeros((local.shape[0], width), jnp.float32)
    for offset in range(4):
        target = (local + offset) % period
        result = result + jnp.where(columns == target[:, None], weights[offset][:, None], 0.0)
    return result


def dft_tables(length):
    counter = lax.iota(jnp.int32, length)
    product = counter[:, None] * counter[None, :] % length
    angle = 2.0 * math.pi / length * product.astype(jnp.float32)
    return (jnp.cos(angle), jnp.sin(angle))


def rotate_pair(real_part, imag_part, pattern, cosine, sine, direction):
    real_cos = jnp.einsum(pattern, real_part, cosine, precision=highest)
    real_sin = jnp.einsum(pattern, real_part, sine, precision=highest)
    imag_cos = jnp.einsum(pattern, imag_part, cosine, precision=highest)
    imag_sin = jnp.einsum(pattern, imag_part, sine, precision=highest)
    return (real_cos - direction * imag_sin, imag_cos + direction * real_sin)


def body(charges, structure_id, live_count, cell_index, fraction, influence):
    atom_total = charges.shape[0]
    row_count = lax.axis_size("row")
    col_count = lax.axis_size("col")
    mesh_x = CX * row_count
    mesh_y = CY * col_count
    structures = S_DEV * row_count * col_count
    local_x = cell_index[0] - lax.axis_index("row") * CX
    local_y = cell_index[1] - lax.axis_index("col") * CY
    live = (lax.iota(jnp.int32, atom_total) < live_count[0]).astype(jnp.float32)
    wx_val, wx_slope = spline_weights(fraction[0])
    wy_val, wy_slope = spline_weights(fraction[1])
    wz_val, wz_slope = spline_weights(fraction[2])
    big_period = 4 * (CX + CY + 8)
    x_rows = place_weights(wx_val, local_x, CX + 3, big_period)
    x_slope_rows = place_weights(wx_slope, local_x, CX + 3, big_period)
    y_rows = place_weights(wy_val, local_y, CY + 3, big_period)
    y_slope_rows = place_weights(wy_slope, local_y, CY + 3, big_period)
    z_rows = place_weights(wz_val, cell_index[2], NZ, NZ)
    z_slope_rows = place_weights(wz_slope, cell_index[2], NZ, NZ)
    plane = (y_rows[:, :, None] * x_rows[:, None, :]).reshape(atom_total, -1)
    charge_sums = jax.ops.segment_sum(charges * live, structure_id, num_segments=structures)
    live_sums = jax.ops.segment_sum(live, structure_id, num_segments=structures)
    totals, counts = lax.psum((charge_sums, live_sums), ("row", "col"))
    neutral = (charges - jnp.take(totals / counts, structure_id)) * live
    spread_grid = lax.dot_general(
        plane,
        neutral[:, None] * z_rows,
        (((0,), (0,)), ((), ())),
        precision=highest,
        preferred_element_type=jnp.float32,
    )
    extended = spread_grid.reshape(CY + 3, CX + 3, NZ)
    spill_x = passed_along(extended[:, CX:, :], "row", 1)
    extended = extended[:, :CX, :].at[:, :3, :].add(spill_x)
    spill_y = passed_along(extended[CY:], "col", 1)
    density = extended[:CY].at[:3].add(spill_y)
    cos_z, sin_z = dft_tables(NZ)
    cos_y, sin_y = dft_tables(mesh_y)
    cos_x, sin_x = dft_tables(mesh_x)
    real_z = jnp.einsum("yxz,zk->kxy", density, cos_z, precision=highest)
    imag_z = -jnp.einsum("yxz,zk->kxy", density, sin_z, precision=highest)
    columns = lax.all_to_all(
        jnp.stack([real_z, imag_z]), "col", split_axis=1, concat_axis=3, tiled=True
    )
    real_y, imag_y = rotate_pair(columns[0], columns[1], "zxy,yk->zkx", cos_y, sin_y, -1.0)
    rows = lax.all_to_all(
        jnp.stack([real_y, imag_y]), "row", split_axis=2, concat_axis=3, tiled=True
    )
    real_x, imag_x = rotate_pair(rows[0], rows[1], "zyx,xk->zyk", cos_x, sin_x, -1.0)
    scale = influence / float(mesh_x * mesh_y * NZ)
    real_x = real_x * scale
    imag_x = imag_x * scale
    back_x, back_x_imag = rotate_pair(real_x, imag_x, "zyk,kx->zyx", cos_x, sin_x, 1.0)
    returned = lax.all_to_all(
        jnp.stack([back_x, back_x_imag]), "row", split_axis=3, concat_axis=2, tiled=True
    )
    back_y, back_y_imag = rotate_pair(returned[0], returned[1], "zkx,ky->zxy", cos_y, sin_y, 1.0)
    whole_z = lax.all_to_all(
        jnp.stack([back_y, back_y_imag]), "col", split_axis=3, concat_axis=1, tiled=True
    )
    potential = jnp.einsum("kxy,kz->yxz", whole_z[0], cos_z, precision=highest) - jnp.einsum(
        "kxy,kz->yxz", whole_z[1], sin_z, precision=highest
    )
    upper_x = passed_along(potential[:, :3, :], "row", -1)
    widened = jnp.concatenate([potential, upper_x], axis=1)
    upper_y = passed_along(widened[:3], "col", -1)
    widened = jnp.concatenate([widened, upper_y], axis=0).reshape(-1, NZ)
    sampled = lax.dot_general(
        jnp.concatenate([z_rows, z_slope_rows], axis=0),
        widened,
        (((1,), (1,)), ((), ())),
        precision=highest,
        preferred_element_type=jnp.float32,
    )
    sample_val = sampled[:atom_total]
    sample_slope = sampled[atom_total:]
    plane_dx = (y_rows[:, :, None] * x_slope_rows[:, None, :]).reshape(atom_total, -1)
    plane_dy = (y_slope_rows[:, :, None] * x_rows[:, None, :]).reshape(atom_total, -1)
    value = jnp.sum(plane * sample_val, axis=1)
    grad_x = jnp.sum(plane_dx * sample_val, axis=1)
    grad_y = jnp.sum(plane_dy * sample_val, axis=1)
    grad_z = jnp.sum(plane * sample_slope, axis=1)
    atom_energy = 0.5 * neutral * value
    forces = -neutral[None, :] * jnp.stack([grad_x, grad_y, grad_z])
    return (forces, atom_energy)


EXT_Y = CY + 3
HALO_ROWS = 24
PLANE = 256
LANES = 128
MESH = pl.DeviceIdType.MESH


def plane_cells():
    cells = np.zeros((PLANE, 2), np.int64)
    used = np.zeros((PLANE,), bool)
    for y in range(EXT_Y):
        for x in range(CX):
            cells[y * CX + x] = (x, y)
            used[y * CX + x] = True
    for x in range(3):
        for y in range(EXT_Y):
            cells[EXT_Y * CX + x * HALO_ROWS + y] = (CX + x, y)
            used[EXT_Y * CX + x * HALO_ROWS + y] = True
    return cells, used


def make_plan(rows, cols):
    n = rows * cols
    offsets = [(0, 0), (1, 0), (-1, 0), (0, 1), (0, -1), (rows // 2, 0)]
    distinct = len({(a % rows, b % cols) for a, b in offsets}) == len(offsets)
    if not (
        rows % 2 == 0
        and cols % 2 == 0
        and distinct
        and NZ % (2 * n) == 0
        and (NZ // n) % 8 == 0
        and NZ % (cols * n) == 0
        and (CY * cols) % rows == 0
        and CY == 2 * rows
        and NZ // cols == 2 * n
        and (NZ // n) * n == PLANE
        and NZ // n // 2 * n == LANES
    ):
        return None
    return (rows, cols, tuple(offsets))


def make_tables(rows, cols):
    n = rows * cols
    half = NZ // n // 2
    slots = 2 * half
    z = np.arange(NZ)
    forward_z = np.zeros((n, 2, half, NZ))
    for p in range(n):
        for j in range(half):
            angle = 2 * np.pi * ((p + n * j) * z % NZ) / NZ
            forward_z[p, 0, j] = np.cos(angle)
            forward_z[p, 1, j] = -np.sin(angle)
    forward_z[0, 1, 0] = 1.0 - 2.0 * (z % 2)
    forward_z = forward_z.reshape(NZ, NZ)

    r, c, m1, k1 = np.meshgrid(
        np.arange(rows), np.arange(cols), np.arange(cols), np.arange(rows), indexing="ij"
    )
    phi = 2 * np.pi * ((k1 * r % rows) / rows + (m1 * c % cols) / cols)
    phi = phi.reshape(n, n)
    cosp, sinp = np.cos(phi), np.sin(phi)
    gather = np.zeros((2, n, 2, half, 2, slots, n))
    for kind in range(2):
        for t in range(slots):
            j, sign = t, 1.0
            if t >= half:
                j, sign = (slots - 1 - t if kind else slots - t), -1.0
            if kind == 0 and t in (0, half):
                part = 0 if t == 0 else 1
                gather[kind, :, part, 0, 0, t] = cosp
                gather[kind, :, part, 0, 1, t] = -sinp
                continue
            gather[kind, :, 0, j, 0, t] = cosp
            gather[kind, :, 1, j, 0, t] = sign * sinp
            gather[kind, :, 0, j, 1, t] = -sinp
            gather[kind, :, 1, j, 1, t] = sign * cosp
    gather = gather.reshape(2, n * 2 * half, 2 * slots * n)

    cells, used = plane_cells()
    x, y = cells[:, 0], cells[:, 1]
    low_m, low_k = (v.reshape(-1) for v in np.meshgrid(np.arange(cols), np.arange(rows), indexing="ij"))
    psi = 2 * np.pi * (
        x[:, None] * low_k[None] / (CX * rows) + y[:, None] * low_m[None] / (CY * cols)
    )
    twiddle = np.stack([np.tile(np.cos(psi), (1, slots)), np.tile(np.sin(psi), (1, slots))])
    high_m, high_k = (v.reshape(-1) for v in np.meshgrid(np.arange(CY), np.arange(CX), indexing="ij"))
    per_row = CY // rows
    order = np.arange(CY * CX).reshape(rows, per_row, CX).transpose(1, 0, 2).reshape(-1)
    high_m, high_k = high_m[order], high_k[order]
    chi = 2 * np.pi * (high_k[:, None] * x[None] % CX / CX + high_m[:, None] * y[None] % CY / CY)
    cosc, sinc = np.cos(chi) * used[None], np.sin(chi) * used[None]
    inner = np.block([[cosc, sinc], [-sinc, cosc]])
    tables = (forward_z, gather, twiddle, inner, inner.T)
    pairs = []
    for table in tables:
        table = np.asarray(table, np.float32)
        high = table.astype(jnp.bfloat16)
        low = (table - high.astype(np.float32)).astype(jnp.bfloat16)
        pairs.append(np.stack([high, low], axis=-3))
    pairs[2] = tables[2].astype(np.float32)
    return tuple(pairs)


def split(values):
    high = values.astype(jnp.bfloat16)
    return high, (values - high.astype(jnp.float32)).astype(jnp.bfloat16)


def dot(left, right, contract):
    def one(a, b):
        return lax.dot_general(
            a, b, ((contract[:1], contract[1:]), ((), ())), preferred_element_type=jnp.float32
        )

    return one(left[0], right[0]) + (one(left[0], right[1]) + one(left[1], right[0]))


def pick(distance, weights):
    result = jnp.where(distance == 3, weights[3], 0.0)
    for i in (2, 1, 0):
        result = jnp.where(distance == i, weights[i], result)
    return result


def kernel(
    plan,
    charges_ref, sid_ref, live_ref, cell_ref, frac_ref, influence_ref,
    fz_hbm, gather_hbm, twiddle_hbm, inner_hbm, inner_t_hbm,
    forces_ref, energy_ref,
    fz, gather, twiddle, inner, inner_t,
    z_rows, z_slopes, plane, x_rows, y_rows,
    frag_out, frag_in, mean_out, mean_in,
    kernel_in, field_out, field_in, back_out, back_in, sampled,
    table_sems, frag_send, frag_recv, mean_send, mean_recv,
    inf_send, inf_recv, field_send, field_recv, back_send, back_recv,
):
    rows, cols, offsets = plan
    n = rows * cols
    r, c = lax.axis_index("row"), lax.axis_index("col")
    me = r * cols + c
    atoms = charges_ref.shape[1]

    def coords(p):
        return (lax.div(p, cols), lax.rem(p, cols))

    barrier = pltpu.get_barrier_semaphore()

    @pl.loop(1, n, unroll=True)
    def _(o):
        pl.semaphore_signal(
            barrier, inc=1, device_id=coords(lax.rem(me + o, n)), device_id_type=MESH
        )

    tables = [
        pltpu.make_async_copy(fz_hbm, fz, table_sems.at[0]),
        pltpu.make_async_copy(gather_hbm.at[jnp.minimum(me, 1)], gather, table_sems.at[1]),
        pltpu.make_async_copy(twiddle_hbm, twiddle, table_sems.at[2]),
        pltpu.make_async_copy(inner_hbm, inner, table_sems.at[3]),
        pltpu.make_async_copy(inner_t_hbm, inner_t, table_sems.at[4]),
    ]
    for table in tables:
        table.start()

    lane = lax.broadcasted_iota(jnp.int32, (1, atoms), 1)
    live = (lane < live_ref[...]).astype(jnp.float32)
    charges = charges_ref[...]
    charged = charges * live
    sid = sid_ref[...]
    within = lax.broadcasted_iota(jnp.int32, (S_DEV, atoms), 0)
    steps = [
        (lax.rem(r + a % rows, rows), lax.rem(c + b % cols, cols)) for a, b in offsets
    ]
    senders = [
        (lax.rem(r + (-a) % rows, rows), lax.rem(c + (-b) % cols, cols)) for a, b in offsets
    ]

    def belongs(o):
        owner = steps[o][0] * cols + steps[o][1]
        return sid == within + owner * S_DEV

    def folded(values):
        total = values[:, :LANES]
        for k in range(1, atoms // LANES):
            total = total + values[:, k * LANES : (k + 1) * LANES]
        return total

    for o in range(len(offsets)):
        mine = belongs(o)
        frag_out[o, :S_DEV] = folded(jnp.where(mine, charged, 0.0))
        frag_out[o, S_DEV:] = folded(jnp.where(mine, live, 0.0))
    pl.semaphore_wait(barrier, n - 1)
    first = [
        pltpu.make_async_remote_copy(
            frag_out.at[o], frag_in.at[o], frag_send.at[o], frag_recv.at[o],
            device_id=steps[o], device_id_type=MESH,
        )
        for o in range(1, len(offsets))
    ]
    for copy in first:
        copy.start()

    place = c * rows + r

    def inf_copy(o):
        p = lax.rem(me + o, n)
        residue = jnp.where(c < cols // 2, p, lax.rem(n - p, n))
        return pltpu.make_async_remote_copy(
            influence_ref.at[residue], kernel_in.at[place], inf_send.at[o], inf_recv.at[o],
            device_id=coords(p), device_id_type=MESH,
        )

    @pl.loop(1, n, unroll=True)
    def _(o):
        inf_copy(o).start()

    own_inf = pltpu.make_async_copy(
        influence_ref.at[jnp.where(c < cols // 2, me, lax.rem(n - me, n))],
        kernel_in.at[place],
        inf_recv.at[0],
    )
    own_inf.start()

    wx, vx = spline_weights(frac_ref[0:1, :])
    wy, vy = spline_weights(frac_ref[1:2, :])
    wz, vz = spline_weights(frac_ref[2:3, :])
    cell_z = cell_ref[2:3, :]
    step = 16

    @pl.loop(0, NZ // step)
    def _(b):
        start = pl.multiple_of(b * step, step)
        index = lax.broadcasted_iota(jnp.int32, (step, atoms), 0) + start - cell_z
        distance = jnp.where(index < 0, index + NZ, index)
        z_rows[0, pl.ds(start, step), :], z_rows[1, pl.ds(start, step), :] = split(
            pick(distance, wz)
        )

    distance = lax.broadcasted_iota(jnp.int32, (16, atoms), 0) - (cell_ref[0:1, :] - r * CX)
    x_rows[0] = pick(distance, wx)
    x_rows[1] = pick(distance, vx)
    distance = lax.broadcasted_iota(jnp.int32, (HALO_ROWS, atoms), 0) - (
        cell_ref[1:2, :] - c * CY
    )
    y_rows[0] = pick(distance, wy)
    y_rows[1] = pick(distance, vy)

    for copy in first:
        copy.wait()
    total = frag_out[0]
    for o in range(1, len(offsets)):
        total = total + frag_in[o]
    charge_sum = jnp.sum(total[:S_DEV], axis=1, keepdims=True)
    live_sum = jnp.sum(total[S_DEV:], axis=1, keepdims=True)
    own_mean = charge_sum / live_sum
    mean_out[...] = jnp.broadcast_to(own_mean, (S_DEV, LANES))
    second = [
        pltpu.make_async_remote_copy(
            mean_out, mean_in.at[o], mean_send.at[o], mean_recv.at[o],
            device_id=senders[o], device_id_type=MESH,
        )
        for o in range(1, len(offsets))
    ]
    for copy in second:
        copy.start()

    @pl.loop(0, NZ // step)
    def _(b):
        start = pl.multiple_of(b * step, step)
        index = lax.broadcasted_iota(jnp.int32, (step, atoms), 0) + start - cell_z
        distance = jnp.where(index < 0, index + NZ, index)
        z_slopes[0, pl.ds(start, step), :], z_slopes[1, pl.ds(start, step), :] = split(
            pick(distance, vz)
        )

    for copy in second:
        copy.wait()
    mean = jnp.where(belongs(0), own_mean, 0.0)
    for o in range(1, len(offsets)):
        mean = mean + jnp.where(belongs(o), mean_in[o][:, 0:1], 0.0)
    mean = jnp.sum(mean, axis=0, keepdims=True)
    neutral = (charges - mean) * live

    x_charged = x_rows[0, :CX] * neutral
    for y in range(EXT_Y):
        plane[y * CX : (y + 1) * CX, :] = y_rows[0, y : y + 1, :] * x_charged
    y_charged = y_rows[0] * neutral
    base = EXT_Y * CX
    for x in range(3):
        plane[base + x * HALO_ROWS : base + (x + 1) * HALO_ROWS, :] = (
            x_rows[0, CX + x : CX + x + 1, :] * y_charged
        )
    top = base + 3 * HALO_ROWS
    plane[top:, :] = jnp.zeros((PLANE - top, atoms), jnp.float32)
    spread = dot((z_rows[0], z_rows[1]), split(plane[...]), (1, 1))
    tables[0].wait()
    field_out[...] = dot((fz[0], fz[1]), split(spread), (1, 0)).reshape(field_out.shape)

    def exchange(source, target, send, recv):
        def copy(o):
            p = lax.rem(me + o, n)
            return pltpu.make_async_remote_copy(
                source.at[p], target.at[me], send.at[o], recv.at[o],
                device_id=coords(p), device_id_type=MESH,
            )

        @pl.loop(1, n, unroll=True)
        def _(o):
            copy(o).start()

        target[me] = source[me]

        @pl.loop(1, n, unroll=True)
        def _(o):
            pltpu.make_async_remote_copy(
                source.at[0], target.at[0], send.at[o], recv.at[o],
                device_id=(r, c), device_id_type=MESH,
            ).wait()

    exchange(field_out, field_in, field_send, field_recv)

    @pl.loop(1, n, unroll=True)
    def _(o):
        pltpu.make_async_remote_copy(
            influence_ref.at[0], kernel_in.at[0], inf_send.at[o], inf_recv.at[o],
            device_id=(r, c), device_id_type=MESH,
        ).wait()

    own_inf.wait()
    for table in tables[1:]:
        table.wait()

    low = dot(split(field_in[...].reshape(PLANE, PLANE).T), (gather[0], gather[1]), (1, 0))
    real, imag = low[:, :NZ], low[:, NZ:]
    cosine, sine = twiddle[0], twiddle[1]
    turned = jnp.concatenate(
        [real * cosine + imag * sine, imag * cosine - real * sine], axis=0
    )
    spectrum = dot((inner[0], inner[1]), split(turned), (1, 0))
    by_col = kernel_in[...].reshape(cols, rows * CX, LANES)
    swapped = [pltpu.roll(by_col[k], LANES // 2, 1) for k in range(cols)]
    first_half = lax.broadcasted_iota(jnp.int32, (rows * CX, LANES), 1) < LANES // 2
    lower = [jnp.where(first_half, by_col[k], swapped[k + 1]) for k in range(0, cols, 2)]
    upper = [jnp.where(first_half, swapped[k], by_col[k + 1]) for k in range(0, cols, 2)]
    green = jnp.concatenate(
        [jnp.concatenate(lower, axis=1), jnp.concatenate(upper, axis=1)], axis=0
    )
    filtered = spectrum * jnp.concatenate([green, green], axis=0)
    back = dot((inner_t[0], inner_t[1]), split(filtered), (1, 0))
    real, imag = back[:PLANE], back[PLANE:]
    turned = jnp.concatenate(
        [real * cosine - imag * sine, imag * cosine + real * sine], axis=1
    )
    back_out[...] = dot((gather[0], gather[1]), split(turned), (1, 1)).reshape(back_out.shape)
    exchange(back_out, back_in, back_send, back_recv)

    scale = 1.0 / float(CX * rows * CY * cols * NZ)
    potential = dot(split(back_in[...].reshape(PLANE, PLANE).T), (fz[0], fz[1]), (1, 0))
    potential = split(potential[:top] * scale)
    sampled[0] = dot(potential, (z_rows[0], z_rows[1]), (1, 0))
    sampled[1] = dot(potential, (z_slopes[0], z_slopes[1]), (1, 0))
    width = 256
    for k in range(atoms // width):
        cut = slice(k * width, (k + 1) * width)
        by_y = by_dy = by_yz = 0.0
        for y in range(EXT_Y):
            row = slice(y * CX, (y + 1) * CX)
            weight = y_rows[0, y : y + 1, cut]
            by_y = by_y + weight * sampled[0, row, cut]
            by_dy = by_dy + y_rows[1, y : y + 1, cut] * sampled[0, row, cut]
            by_yz = by_yz + weight * sampled[1, row, cut]
        by_x = by_dx = by_xz = 0.0
        for x in range(3):
            row = slice(base + x * HALO_ROWS, base + (x + 1) * HALO_ROWS)
            weight = x_rows[0, CX + x : CX + x + 1, cut]
            by_x = by_x + weight * sampled[0, row, cut]
            by_dx = by_dx + x_rows[1, CX + x : CX + x + 1, cut] * sampled[0, row, cut]
            by_xz = by_xz + weight * sampled[1, row, cut]
        xs, dxs = x_rows[0, :CX, cut], x_rows[1, :CX, cut]
        ys, dys = y_rows[0, :, cut], y_rows[1, :, cut]

        def down(values):
            return jnp.sum(values, axis=0, keepdims=True)

        value = down(xs * by_y) + down(ys * by_x)
        grad_x = down(dxs * by_y) + down(ys * by_dx)
        grad_y = down(xs * by_dy) + down(dys * by_x)
        grad_z = down(xs * by_yz) + down(ys * by_xz)
        part = neutral[:, cut]
        energy_ref[:, cut] = 0.5 * part * value
        forces_ref[0:1, cut] = -part * grad_x
        forces_ref[1:2, cut] = -part * grad_y
        forces_ref[2:3, cut] = -part * grad_z


def fast_body(plan, charges, structure_id, live_count, cell_index, fraction, influence):
    rows, cols, offsets = plan
    n = rows * cols
    atoms = charges.shape[0]
    per_col = NZ // cols // n
    high = CY // rows
    stored = influence.reshape(per_col, n, high, cols, CX, rows)
    stored = stored.transpose(1, 4, 2, 0, 3, 5).reshape(n, CX, high * per_col * n)
    tables = make_tables(rows, cols)
    vmem = pl.BlockSpec(memory_space=pltpu.VMEM)
    anywhere = pl.BlockSpec(memory_space=pltpu.HBM)
    f32 = jnp.float32
    lines = NZ // n
    count = len(offsets)
    sems = pltpu.SemaphoreType.DMA
    forces, energy = pl.pallas_call(
        functools.partial(kernel, plan),
        out_shape=(
            jax.ShapeDtypeStruct((3, atoms), f32),
            jax.ShapeDtypeStruct((1, atoms), f32),
        ),
        in_specs=[vmem] * 5 + [anywhere] * 6,
        out_specs=(vmem, vmem),
        scratch_shapes=[
            pltpu.VMEM(tables[0].shape, jnp.bfloat16),
            pltpu.VMEM(tables[1].shape[1:], jnp.bfloat16),
            pltpu.VMEM(tables[2].shape, f32),
            pltpu.VMEM(tables[3].shape, jnp.bfloat16),
            pltpu.VMEM(tables[4].shape, jnp.bfloat16),
            pltpu.VMEM((2, NZ, atoms), jnp.bfloat16),
            pltpu.VMEM((2, NZ, atoms), jnp.bfloat16),
            pltpu.VMEM((PLANE, atoms), f32),
            pltpu.VMEM((2, 16, atoms), f32),
            pltpu.VMEM((2, HALO_ROWS, atoms), f32),
            pltpu.VMEM((count, 2 * S_DEV, LANES), f32),
            pltpu.VMEM((count, 2 * S_DEV, LANES), f32),
            pltpu.VMEM((S_DEV, LANES), f32),
            pltpu.VMEM((count, S_DEV, LANES), f32),
            pltpu.VMEM((n, CX, LANES), f32),
            pltpu.VMEM((n, lines, PLANE), f32),
            pltpu.VMEM((n, lines, PLANE), f32),
            pltpu.VMEM((n, lines, PLANE), f32),
            pltpu.VMEM((n, lines, PLANE), f32),
            pltpu.VMEM((2, EXT_Y * CX + 3 * HALO_ROWS, atoms), f32),
            sems((5,)),
            sems((count,)), sems((count,)), sems((count,)), sems((count,)),
            sems((n,)), sems((n,)), sems((n,)), sems((n,)), sems((n,)), sems((n,)),
        ],
        compiler_params=pltpu.CompilerParams(
            collective_id=0, has_side_effects=True, vmem_limit_bytes=48 * 1024 * 1024
        ),
        name="ewald_step",
    )(
        charges[None, :], structure_id[None, :], live_count[None, :], cell_index, fraction, stored,
        *[jnp.asarray(t) for t in tables],
    )
    return forces, energy[0]


def solution(mesh):
    plan = make_plan(mesh.shape["row"], mesh.shape["col"])
    placed = (
        P(("row", "col")),
        P(("row", "col")),
        P(("row", "col")),
        P(None, ("row", "col")),
        P(None, ("row", "col")),
        P("col", "row", None),
    )
    return jax.shard_map(
        body if plan is None else functools.partial(fast_body, plan),
        mesh=mesh,
        in_specs=placed,
        out_specs=(P(None, ("row", "col")), P(("row", "col"))),
        check_vma=False,
    )
```

profile of v0, /device:TPU:0, one launch (start us, length us, event | category | flops | bytes accessed | tf_op | source)
XLA Modules:
  0.0 39.6 jit_solution(3168577265088093614)
XLA Ops:
  0.6 0.0 copy-start.3
  0.6 1.1 %copy.14 = f32[64,8,64]{0,2,1:T(8,128)S(1)} copy(f32[64,8,64]{2,1,0:T(8,128)} %param.16) | data formatting | bytes 262144 | tf_op args[5]
  1.8 0.0 copy-start.2
  1.8 0.0 copy-start.4
  1.8 0.3 reshape.10
  2.1 0.0 copy-start
  2.2 0.9 %copy.15 = f32[32,8,2,2,4,8]{0,5,4,3,2,1:T(8,128)} copy(f32[32,8,2,2,4,8]{0,3,5,1,4,2:T(2,128)S(1)} %bitcast.13) | data formatting | bytes 262144 | tf_op jit(solution)/shard_map/transpose | solution.py:561
  3.0 0.0 copy-start.1
  3.0 0.0 copy-start.5
  3.0 0.0 copy-start.6
  3.0 1.3 %copy.16.influence_ref = f32[32,8,128]{2,1,0:T(8,128)S(1)} copy(f32[32,8,128]{0,2,1:T(8,128)} %bitcast.12) | data formatting | bytes 262144 | tf_op jit(solution)/shard_map/reshape | solution.py:561
  4.3 0.0 copy-start.7
  5.0 0.0 copy-done.3
  5.0 0.0 copy-done.2
  5.0 0.0 copy-done.4
  5.0 0.0 copy-done
  5.0 0.0 copy-done.1
  5.0 0.0 copy-done.5
  5.0 0.0 copy-done.6
  5.1 0.0 copy-done.8
  5.1 0.0 copy-done.7
  5.1 33.3 %ewald_step.1 = (f32[3,1024]{1,0:T(4,128)S(1)}, f32[1,1024]{1,0:T(1,128)S(1)}) custom-call(f32[1,1024]{1,0:T(1,128)S(1)} %bitcast.9, s32[1,1024]{1,0:T(1,128)S(1)} %bitcast.10, s32[1,1]{1,0:T(1,128)} %bitcast.8.live_ref, s32[3,1024]{1,0:T(4,128)S(1)} %copy-done.5, f32[3,1024]{1,0:T(4,128)S(1)} %copy-done.6, f32[32,8,128]{2,1,0:T(8,128)S(1)} %copy.16.influence_ref, ...), custom_call_target="tpu_custom_call" | custom-call | tf_op jit(solution)/shard_map/ewald_step/pallas_call | solution.py:569
  38.4 0.6 %copy.20 = f32[3,1024]{1,0:T(4,128)} copy(f32[3,1024]{1,0:T(4,128)S(1)} %get-tuple-element.8) | data formatting | bytes 24576
  39.0 0.6 %copy.21 = f32[1024]{0:T(1024)} copy(f32[1024]{0:T(1024)S(1)} %bitcast.11) | data formatting | bytes 8192
  (1 shorter events, 0.0 us)
Async XLA Ops:
  0.6 4.4 %copy-start.3 = (bf16[2,512,256]{2,1,0:T(8,128)(2,1)S(1)}, bf16[2,512,256]{2,1,0:T(8,128)(2,1)}, u32[]{:S(2)}) copy-start(bf16[2,512,256]{2,1,0:T(8,128)(2,1)} %constant.14.clone.inner_t_hbm) | copy-start | bytes 1572868
  1.8 3.2 %copy-start.2 = (bf16[2,256,512]{2,1,0:T(8,128)(2,1)S(1)}, bf16[2,256,512]{2,1,0:T(8,128)(2,1)}, u32[]{:S(2)}) copy-start(bf16[2,256,512]{2,1,0:T(8,128)(2,1)} %constant.13.clone.inner_hbm) | copy-start | bytes 1572868
  1.8 3.2 %copy-start.4 = (bf16[2,256,256]{2,1,0:T(8,128)(2,1)S(1)}, bf16[2,256,256]{2,1,0:T(8,128)(2,1)}, u32[]{:S(2)}) copy-start(bf16[2,256,256]{2,1,0:T(8,128)(2,1)} %constant.10.clone.fz_hbm) | copy-start | bytes 786436
  2.1 2.9 %copy-start = (bf16[2,2,256,512]{3,2,1,0:T(8,128)(2,1)S(1)}, bf16[2,2,256,512]{3,2,1,0:T(8,128)(2,1)}, u32[]{:S(2)}) copy-start(bf16[2,2,256,512]{3,2,1,0:T(8,128)(2,1)} %constant.11.clone.gather_hbm) | copy-start | bytes 3145732
  3.0 2.0 %copy-start.1 = (f32[2,256,256]{2,1,0:T(8,128)S(1)}, f32[2,256,256]{2,1,0:T(8,128)}, u32[]{:S(2)}) copy-start(f32[2,256,256]{2,1,0:T(8,128)} %constant.12.clone.twiddle_hbm) | copy-start | bytes 1572868
  3.0 2.0 %copy-start.5 = (s32[3,1024]{1,0:T(4,128)S(1)}, s32[3,1024]{1,0:T(4,128)}, u32[]{:S(2)}) copy-start(s32[3,1024]{1,0:T(4,128)} %cell_ref.1) | copy-start | bytes 36868
  3.0 2.0 %copy-start.6 = (f32[3,1024]{1,0:T(4,128)S(1)}, f32[3,1024]{1,0:T(4,128)}, u32[]{:S(2)}) copy-start(f32[3,1024]{1,0:T(4,128)} %frac_ref.1) | copy-start | bytes 36868
  3.0 2.0 %copy-start.8 = (s32[1024]{0:T(1024)S(1)}, s32[1024]{0:T(1024)}, u32[]{:S(2)}) copy-start(s32[1024]{0:T(1024)} %param.12) | copy-start | bytes 12292
  4.3 0.8 %copy-start.7 = (f32[1024]{0:T(1024)S(1)}, f32[1024]{0:T(1024)}, u32[]{:S(2)}) copy-start(f32[1024]{0:T(1024)} %param.11) | copy-start | bytes 12292
where the time goes:
time: 40.1 us; the launch traced here: 39.6 us
  Pallas kernels  33.3 us (83%)
  local copies, waits for them, and re-layouts  4.85 us (12%)
  between operations  1.44 us (4%)
    pallas_call x1, Pallas kernels, fast_body(): pl.pallas_call(functools.partial(kernel, plan), out_shape=(jax.ShapeDtype...  33.3 us
    unnamed x21, local copies, waits for them, and re-layouts  2.39 us
    reshape x1, local copies, waits for them, and re-layouts, fast_body(): stored.transpose(1, 4, 2, 0, 3, 5).reshape(n, CX, high * per_col * n)  1.28 us
    transpose x1, local copies, waits for them, and re-layouts, fast_body(): stored.transpose(1, 4, 2, 0, 3, 5).reshape(n, CX, high * per_col * n)  0.87 us

commit v1 on v0

v1 whole, which is shorter than its diff:
```python
import math

import functools

import jax
import jax.numpy as jnp
import numpy as np
from jax import lax
from jax.experimental import pallas as pl
from jax.experimental.pallas import tpu as pltpu
from jax.sharding import PartitionSpec as P

CX = 8
CY = 16
NZ = 256
S_DEV = 8


highest = lax.Precision.HIGHEST


def passed_along(block, axis, distance):
    devices = range(lax.axis_size(axis))
    route = [((i - distance) % len(devices), i) for i in devices]
    return lax.ppermute(block, axis, route)


def spline_weights(fraction):
    remain = 1.0 - fraction
    square = fraction * fraction
    cubic_term = square * fraction
    values = [
        remain * remain * remain / 6.0,
        (3.0 * cubic_term - 6.0 * square + 4.0) / 6.0,
        (-3.0 * cubic_term + 3.0 * square + 3.0 * fraction + 1.0) / 6.0,
        cubic_term / 6.0,
    ]
    slopes = [
        -0.5 * remain * remain,
        0.5 * (3.0 * square - 4.0 * fraction),
        0.5 * (-3.0 * square + 2.0 * fraction + 1.0),
        0.5 * square,
    ]
    return (values, slopes)


def place_weights(weights, local, width, period):
    columns = lax.broadcasted_iota(jnp.int32, (local.shape[0], width), 1)
    result = jnp.zeros((local.shape[0], width), jnp.float32)
    for offset in range(4):
        target = (local + offset) % period
        result = result + jnp.where(columns == target[:, None], weights[offset][:, None], 0.0)
    return result


def dft_tables(length):
    counter = lax.iota(jnp.int32, length)
    product = counter[:, None] * counter[None, :] % length
    angle = 2.0 * math.pi / length * product.astype(jnp.float32)
    return (jnp.cos(angle), jnp.sin(angle))


def rotate_pair(real_part, imag_part, pattern, cosine, sine, direction):
    real_cos = jnp.einsum(pattern, real_part, cosine, precision=highest)
    real_sin = jnp.einsum(pattern, real_part, sine, precision=highest)
    imag_cos = jnp.einsum(pattern, imag_part, cosine, precision=highest)
    imag_sin = jnp.einsum(pattern, imag_part, sine, precision=highest)
    return (real_cos - direction * imag_sin, imag_cos + direction * real_sin)


def body(charges, structure_id, live_count, cell_index, fraction, influence):
    atom_total = charges.shape[0]
    row_count = lax.axis_size("row")
    col_count = lax.axis_size("col")
    mesh_x = CX * row_count
    mesh_y = CY * col_count
    structures = S_DEV * row_count * col_count
    local_x = cell_index[0] - lax.axis_index("row") * CX
    local_y = cell_index[1] - lax.axis_index("col") * CY
    live = (lax.iota(jnp.int32, atom_total) < live_count[0]).astype(jnp.float32)
    wx_val, wx_slope = spline_weights(fraction[0])
    wy_val, wy_slope = spline_weights(fraction[1])
    wz_val, wz_slope = spline_weights(fraction[2])
    big_period = 4 * (CX + CY + 8)
    x_rows = place_weights(wx_val, local_x, CX + 3, big_period)
    x_slope_rows = place_weights(wx_slope, local_x, CX + 3, big_period)
    y_rows = place_weights(wy_val, local_y, CY + 3, big_period)
    y_slope_rows = place_weights(wy_slope, local_y, CY + 3, big_period)
    z_rows = place_weights(wz_val, cell_index[2], NZ, NZ)
    z_slope_rows = place_weights(wz_slope, cell_index[2], NZ, NZ)
    plane = (y_rows[:, :, None] * x_rows[:, None, :]).reshape(atom_total, -1)
    charge_sums = jax.ops.segment_sum(charges * live, structure_id, num_segments=structures)
    live_sums = jax.ops.segment_sum(live, structure_id, num_segments=structures)
    totals, counts = lax.psum((charge_sums, live_sums), ("row", "col"))
    neutral = (charges - jnp.take(totals / counts, structure_id)) * live
    spread_grid = lax.dot_general(
        plane,
        neutral[:, None] * z_rows,
        (((0,), (0,)), ((), ())),
        precision=highest,
        preferred_element_type=jnp.float32,
    )
    extended = spread_grid.reshape(CY + 3, CX + 3, NZ)
    spill_x = passed_along(extended[:, CX:, :], "row", 1)
    extended = extended[:, :CX, :].at[:, :3, :].add(spill_x)
    spill_y = passed_along(extended[CY:], "col", 1)
    density = extended[:CY].at[:3].add(spill_y)
    cos_z, sin_z = dft_tables(NZ)
    cos_y, sin_y = dft_tables(mesh_y)
    cos_x, sin_x = dft_tables(mesh_x)
    real_z = jnp.einsum("yxz,zk->kxy", density, cos_z, precision=highest)
    imag_z = -jnp.einsum("yxz,zk->kxy", density, sin_z, precision=highest)
    columns = lax.all_to_all(
        jnp.stack([real_z, imag_z]), "col", split_axis=1, concat_axis=3, tiled=True
    )
    real_y, imag_y = rotate_pair(columns[0], columns[1], "zxy,yk->zkx", cos_y, sin_y, -1.0)
    rows = lax.all_to_all(
        jnp.stack([real_y, imag_y]), "row", split_axis=2, concat_axis=3, tiled=True
    )
    real_x, imag_x = rotate_pair(rows[0], rows[1], "zyx,xk->zyk", cos_x, sin_x, -1.0)
    scale = influence / float(mesh_x * mesh_y * NZ)
    real_x = real_x * scale
    imag_x = imag_x * scale
    back_x, back_x_imag = rotate_pair(real_x, imag_x, "zyk,kx->zyx", cos_x, sin_x, 1.0)
    returned = lax.all_to_all(
        jnp.stack([back_x, back_x_imag]), "row", split_axis=3, concat_axis=2, tiled=True
    )
    back_y, back_y_imag = rotate_pair(returned[0], returned[1], "zkx,ky->zxy", cos_y, sin_y, 1.0)
    whole_z = lax.all_to_all(
        jnp.stack([back_y, back_y_imag]), "col", split_axis=3, concat_axis=1, tiled=True
    )
    potential = jnp.einsum("kxy,kz->yxz", whole_z[0], cos_z, precision=highest) - jnp.einsum(
        "kxy,kz->yxz", whole_z[1], sin_z, precision=highest
    )
    upper_x = passed_along(potential[:, :3, :], "row", -1)
    widened = jnp.concatenate([potential, upper_x], axis=1)
    upper_y = passed_along(widened[:3], "col", -1)
    widened = jnp.concatenate([widened, upper_y], axis=0).reshape(-1, NZ)
    sampled = lax.dot_general(
        jnp.concatenate([z_rows, z_slope_rows], axis=0),
        widened,
        (((1,), (1,)), ((), ())),
        precision=highest,
        preferred_element_type=jnp.float32,
    )
    sample_val = sampled[:atom_total]
    sample_slope = sampled[atom_total:]
    plane_dx = (y_rows[:, :, None] * x_slope_rows[:, None, :]).reshape(atom_total, -1)
    plane_dy = (y_slope_rows[:, :, None] * x_rows[:, None, :]).reshape(atom_total, -1)
    value = jnp.sum(plane * sample_val, axis=1)
    grad_x = jnp.sum(plane_dx * sample_val, axis=1)
    grad_y = jnp.sum(plane_dy * sample_val, axis=1)
    grad_z = jnp.sum(plane * sample_slope, axis=1)
    atom_energy = 0.5 * neutral * value
    forces = -neutral[None, :] * jnp.stack([grad_x, grad_y, grad_z])
    return (forces, atom_energy)


EXT_Y = CY + 3
HALO_ROWS = 24
PLANE = 256
LANES = 128
TOP = EXT_Y * CX + 3 * HALO_ROWS
CHUNKS = 2
MESH = pl.DeviceIdType.MESH


def plane_cells():
    cells = np.zeros((PLANE, 2), np.int64)
    used = np.zeros((PLANE,), bool)
    for y in range(EXT_Y):
        for x in range(CX):
            cells[y * CX + x] = (x, y)
            used[y * CX + x] = True
    for x in range(3):
        for y in range(EXT_Y):
            cells[EXT_Y * CX + x * HALO_ROWS + y] = (CX + x, y)
            used[EXT_Y * CX + x * HALO_ROWS + y] = True
    return cells, used


def make_plan(rows, cols):
    n = rows * cols
    offsets = [(0, 0), (1, 0), (-1, 0), (0, 1), (0, -1), (rows // 2, 0)]
    distinct = len({(a % rows, b % cols) for a, b in offsets}) == len(offsets)
    if not (
        rows % 2 == 0
        and cols % 2 == 0
        and rows & (rows - 1) == 0
        and cols & (cols - 1) == 0
        and distinct
        and (CY * cols) % rows == 0
        and CY == 2 * rows
        and CX == 8
        and NZ == 8 * n
        and NZ // cols == 2 * n
        and 4 * n == LANES
        and cols == 4
    ):
        return None
    diffs = [(0, 0)]
    for a, b in offsets:
        for d, e in offsets:
            diff = ((a - d) % rows, (b - e) % cols)
            if diff not in diffs:
                diffs.append(diff)
    return (rows, cols, tuple(offsets), tuple(diffs))


def slot_lists(kind):
    if kind:
        return ((0, 1, 6, 7), (2, 3, 4, 5))
    return ((0, 1, 4, 7), (2, 3, 5, 6))


def make_tables(rows, cols):
    n = rows * cols
    half = NZ // n // 2
    slots = 2 * half
    z = np.arange(NZ)
    forward_z = np.zeros((n, 2, half, NZ))
    for p in range(n):
        for j in range(half):
            angle = 2 * np.pi * ((p + n * j) * z % NZ) / NZ
            forward_z[p, 0, j] = np.cos(angle)
            forward_z[p, 1, j] = -np.sin(angle)
    forward_z[0, 1, 0] = 1.0 - 2.0 * (z % 2)
    per_chunk = half // CHUNKS
    forward_z = forward_z.reshape(n, 2, CHUNKS, per_chunk, NZ).transpose(2, 0, 1, 3, 4)
    forward_z = forward_z.reshape(NZ, NZ)

    r, c, m1, k1 = np.meshgrid(
        np.arange(rows), np.arange(cols), np.arange(cols), np.arange(rows), indexing="ij"
    )
    phi = 2 * np.pi * ((k1 * r % rows) / rows + (m1 * c % cols) / cols)
    phi = phi.reshape(n, n)
    cosp, sinp = np.cos(phi), np.sin(phi)
    gather = np.zeros((2, n, 2, half, 2, slots, n))
    for kind in range(2):
        for t in range(slots):
            j, sign = t, 1.0
            if t >= half:
                j, sign = (slots - 1 - t if kind else slots - t), -1.0
            if kind == 0 and t in (0, half):
                part = 0 if t == 0 else 1
                gather[kind, :, part, 0, 0, t] = cosp
                gather[kind, :, part, 0, 1, t] = -sinp
                continue
            gather[kind, :, 0, j, 0, t] = cosp
            gather[kind, :, 1, j, 0, t] = sign * sinp
            gather[kind, :, 0, j, 1, t] = -sinp
            gather[kind, :, 1, j, 1, t] = sign * cosp
    chunked = np.zeros((2, CHUNKS, n, 2, per_chunk, 2, slots // CHUNKS, n))
    for kind in range(2):
        for ch in range(CHUNKS):
            js = slice(ch * per_chunk, (ch + 1) * per_chunk)
            chunked[kind, ch] = gather[kind][:, :, js][:, :, :, :, list(slot_lists(kind)[ch])]
    lines = 2 * per_chunk * n
    gather = chunked.reshape(2, CHUNKS, lines, slots * n)

    cells, used = plane_cells()
    x, y = cells[:, 0], cells[:, 1]
    low_m, low_k = (v.reshape(-1) for v in np.meshgrid(np.arange(cols), np.arange(rows), indexing="ij"))
    psi = 2 * np.pi * (
        x[None] * low_k[:, None] / (CX * rows) + y[None] * low_m[:, None] / (CY * cols)
    )
    twiddle = np.stack([np.cos(psi), np.sin(psi)])
    high_m, high_k = (v.reshape(-1) for v in np.meshgrid(np.arange(CY), np.arange(CX), indexing="ij"))
    chi = 2 * np.pi * (high_k[:, None] * x[None] % CX / CX + high_m[:, None] * y[None] % CY / CY)
    cosc, sinc = np.cos(chi) * used[None], np.sin(chi) * used[None]
    inner = np.block([[cosc, sinc], [-sinc, cosc]])
    width = CX * rows
    source = np.arange(rows * 2 * width)
    spot = (source // width) * CX + source % width // rows
    place = (spot[:, None] == np.arange(CY * CX)[None]).astype(np.float32)

    def pair(table, axis):
        table = np.asarray(table, np.float32)
        high = table.astype(jnp.bfloat16)
        low = (table - high.astype(np.float32)).astype(jnp.bfloat16)
        return np.stack([high, low], axis=axis)

    turned = gather.transpose(0, 1, 3, 2)
    wide = np.concatenate(list(pair(turned, 0)), axis=-1)
    return (
        pair(forward_z, 0),
        wide,
        pair(gather, 2),
        twiddle.astype(np.float32),
        pair(inner.T, 0),
        pair(inner, 0),
        place.astype(jnp.bfloat16),
    )


def split(values):
    high = values.astype(jnp.bfloat16)
    return high, (values - high.astype(jnp.float32)).astype(jnp.bfloat16)


def one_dot(a, b, contract=(1, 0)):
    return lax.dot_general(
        a, b, ((contract[:1], contract[1:]), ((), ())), preferred_element_type=jnp.float32
    )


def dot(left, right, contract=(1, 0)):
    return one_dot(left[0], right[0], contract) + (
        one_dot(left[0], right[1], contract) + one_dot(left[1], right[0], contract)
    )


def pick(distance, weights):
    result = jnp.where(distance == 3, weights[3], 0.0)
    for i in (2, 1, 0):
        result = jnp.where(distance == i, weights[i], result)
    return result


def kernel(
    plan,
    charges_hbm, sid_hbm, live_hbm, cell_hbm, frac_hbm, influence_hbm,
    fz_hbm, wide_hbm, gather_hbm, twiddle_hbm, inner_t_hbm, inner_hbm, place_hbm,
    forces_ref, energy_ref,
    charges_ref, sid_ref, live_ref, cell_ref, frac_ref, raw,
    fz, wide, gather, twiddle, inner_t, inner, spot,
    z_rows, z_slopes, zf, plane, x_rows, y_rows,
    frag, inf_out, inf_in, green,
    field_out, field_in, back_out, back_in, sampled,
    local_sems, frag_send, frag_recv, inf_send, inf_recv, send_sems, recv_sems,
):
    rows, cols, offsets, diffs = plan
    n = rows * cols
    r, c = lax.axis_index("row"), lax.axis_index("col")
    me = r * cols + c
    atoms = charges_ref.shape[1]
    lines = NZ // CHUNKS
    kind = jnp.minimum(me, 1)
    far_first = sorted(range(1, n), key=lambda o: -o)

    def peer(o):
        return (r ^ (o // cols), c ^ (o % cols))

    barrier = pltpu.get_barrier_semaphore()
    for o in far_first:
        pl.semaphore_signal(barrier, inc=1, device_id=peer(o), device_id_type=MESH)

    copies = [
        pltpu.make_async_copy(source, target, local_sems.at[i])
        for i, (source, target) in enumerate([
            (charges_hbm, charges_ref),
            (sid_hbm, sid_ref),
            (live_hbm, live_ref),
            (frac_hbm, frac_ref),
            (cell_hbm, cell_ref),
            (influence_hbm, raw),
            (fz_hbm, fz),
            (wide_hbm.at[kind], wide),
            (gather_hbm.at[kind], gather),
            (twiddle_hbm, twiddle),
            (inner_t_hbm, inner_t),
            (inner_hbm, inner),
            (place_hbm, spot),
        ])
    ]
    for copy in copies:
        copy.start()

    for copy in copies[:3]:
        copy.wait()
    lane = lax.broadcasted_iota(jnp.int32, (1, atoms), 1)
    live = (lane < live_ref[0]).astype(jnp.float32)
    charges = charges_ref[...]
    charged = charges * live
    sid = sid_ref[...]
    within = lax.broadcasted_iota(jnp.int32, (S_DEV, atoms), 0)
    owners = [
        lax.rem(r + a % rows, rows) * cols + lax.rem(c + b % cols, cols) for a, b in offsets
    ]

    def belongs(o):
        return sid == within + owners[o] * S_DEV

    def folded(values):
        total = values[:, :LANES]
        for k in range(1, atoms // LANES):
            total = total + values[:, k * LANES : (k + 1) * LANES]
        return jnp.sum(total, axis=1, keepdims=True)

    tile_lane = lax.broadcasted_iota(jnp.int32, (S_DEV, LANES), 1)
    message = jnp.zeros((S_DEV, LANES), jnp.float32)
    for o in range(len(offsets)):
        mine = belongs(o)
        message = jnp.where(tile_lane == 2 * o, folded(jnp.where(mine, charged, 0.0)), message)
        message = jnp.where(tile_lane == 2 * o + 1, folded(jnp.where(mine, live, 0.0)), message)
    frag[0] = message

    for copy in copies[3:5]:
        copy.wait()
    wx, vx = spline_weights(frac_ref[0:1, :])
    wy, vy = spline_weights(frac_ref[1:2, :])
    wz, vz = spline_weights(frac_ref[2:3, :])
    cell_z = cell_ref[2:3, :]
    step = 16

    def fill(target, weights):
        @pl.loop(0, NZ // step)
        def _(b):
            start = pl.multiple_of(b * step, step)
            index = lax.broadcasted_iota(jnp.int32, (step, atoms), 0) + start - cell_z
            distance = jnp.where(index < 0, index + NZ, index)
            target[0, pl.ds(start, step), :], target[1, pl.ds(start, step), :] = split(
                pick(distance, weights)
            )

    width = 256

    def transform(which, source):
        for k in range(atoms // width):
            cut = slice(k * width, (k + 1) * width)
            value = dot((fz[0], fz[1]), (source[0, :, cut], source[1, :, cut]))
            zf[which, 0, :, cut], zf[which, 1, :, cut] = split(value)

    fill(z_rows, wz)
    copies[6].wait()
    transform(0, z_rows)

    copies[5].wait()
    for p in range(n):
        first, second = raw[0, p], raw[1, p]
        low = jnp.concatenate([first[:4], second[:4]], axis=0)
        high = jnp.concatenate([first[4:], second[4:]], axis=0)
        inf_out[p] = jnp.concatenate([low, high], axis=1)

    pl.semaphore_wait(barrier, n - 1)

    def frag_copy(k):
        a, b = diffs[k]
        target = (lax.rem(r + (-a) % rows, rows), lax.rem(c + (-b) % cols, cols))
        return pltpu.make_async_remote_copy(
            frag.at[0], frag.at[k], frag_send.at[k], frag_recv.at[k],
            device_id=target, device_id_type=MESH,
        )

    frags = [frag_copy(k) for k in range(1, len(diffs))]
    for copy in frags:
        copy.start()

    place = c * rows + r

    def residue(p):
        return jnp.where(c < cols // 2, p, lax.rem(n - p, n))

    for o in far_first:
        pltpu.make_async_remote_copy(
            inf_out.at[residue(me ^ o)], inf_in.at[place], inf_send, inf_recv,
            device_id=peer(o), device_id_type=MESH,
        ).start()
    inf_in[place] = inf_out[residue(me)]

    fill(z_slopes, vz)
    transform(1, z_slopes)
    distance = lax.broadcasted_iota(jnp.int32, (16, atoms), 0) - (cell_ref[0:1, :] - r * CX)
    x_rows[0] = pick(distance, wx)
    x_rows[1] = pick(distance, vx)
    distance = lax.broadcasted_iota(jnp.int32, (HALO_ROWS, atoms), 0) - (
        cell_ref[1:2, :] - c * CY
    )
    y_rows[0] = pick(distance, wy)
    y_rows[1] = pick(distance, vy)
    plane[:, TOP:, :] = jnp.zeros((2, PLANE - TOP, atoms), jnp.bfloat16)

    for copy in frags:
        copy.wait()
    slot = {diff: k for k, diff in enumerate(diffs)}
    mean = jnp.zeros((S_DEV, atoms), jnp.float32)
    for j, (a, b) in enumerate(offsets):
        total = jnp.zeros((S_DEV, LANES), jnp.float32)
        for i, (d, e) in enumerate(offsets):
            part = frag[slot[((a - d) % rows, (b - e) % cols)]]
            total = total + jnp.where(tile_lane // 2 == i, part, 0.0)
        odd = tile_lane % 2 == 1
        charge_sum = jnp.sum(jnp.where(odd, 0.0, total), axis=1, keepdims=True)
        live_sum = jnp.sum(jnp.where(odd, total, 0.0), axis=1, keepdims=True)
        mean = jnp.where(belongs(j), charge_sum / live_sum, mean)
    mean = jnp.sum(mean, axis=0, keepdims=True)
    neutral = (charges - mean) * live

    x_charged = x_rows[0, :CX] * neutral
    for y in range(0, EXT_Y - 1, 2):
        pair = jnp.concatenate(
            [y_rows[0, y : y + 1, :] * x_charged, y_rows[0, y + 1 : y + 2, :] * x_charged], axis=0
        )
        plane[0, y * CX : (y + 2) * CX, :], plane[1, y * CX : (y + 2) * CX, :] = split(pair)
    base = EXT_Y * CX
    y_charged = y_rows[0] * neutral
    tail = [y_rows[0, EXT_Y - 1 : EXT_Y, :] * x_charged]
    for x in range(3):
        tail.append(x_rows[0, CX + x : CX + x + 1, :] * y_charged)
    tail = jnp.concatenate(tail, axis=0)
    plane[0, base - CX : TOP, :], plane[1, base - CX : TOP, :] = split(tail)

    sub_low = lax.broadcasted_iota(jnp.int32, (8, LANES), 0) < 4

    def interleaved(values, target):
        for v in range(n // 2):
            rows8 = slice(8 * v, 8 * v + 8)
            near, far = values[rows8, :LANES], values[rows8, LANES:]
            target[2 * v] = jnp.where(sub_low, near, pltpu.roll(far, 4, 0))
            target[2 * v + 1] = jnp.where(sub_low, pltpu.roll(near, 4, 0), far)

    def gathered(source):
        near, far = [], []
        for v in range(n // 2):
            first, second = source[2 * v], source[2 * v + 1]
            near.append(jnp.where(sub_low, first, pltpu.roll(second, 4, 0)))
            far.append(jnp.where(sub_low, pltpu.roll(first, 4, 0), second))
        return jnp.concatenate(
            [jnp.concatenate(near, axis=0), jnp.concatenate(far, axis=0)], axis=1
        )

    def send(source, target, index):
        for o in far_first:
            pltpu.make_async_remote_copy(
                source.at[me ^ o], target.at[me], send_sems.at[index], recv_sems.at[index],
                device_id=peer(o), device_id_type=MESH,
            ).start()
        target[me] = source[me]

    def whole(source, target, send_sem, recv_sem):
        return pltpu.make_async_remote_copy(
            source.at[pl.ds(0, n - 1)], target.at[pl.ds(0, n - 1)], send_sem, recv_sem,
            device_id=(r, c), device_id_type=MESH,
        )

    for ch in range(CHUNKS):
        mine = slice(ch * lines, (ch + 1) * lines)
        value = dot((zf[0, 0, mine], zf[0, 1, mine]), (plane[0], plane[1]), (1, 1))
        interleaved(value, field_out.at[ch])
        send(field_out.at[ch], field_in.at[ch], ch)

    whole(inf_out, inf_in, inf_send, inf_recv).wait()
    copies[12].wait()
    group = lax.broadcasted_iota(jnp.int32, (8, LANES), 1) % rows
    wanted = group == lax.broadcasted_iota(jnp.int32, (8, LANES), 0)
    for t in range(8):
        blocks = []
        for m in range(cols):
            row = (t % 2) * cols + m
            blocks.append(jnp.concatenate(
                [
                    jnp.where(wanted, inf_in[t // 2 * rows + q, row : row + 1, :], 0.0)
                    for q in range(rows)
                ],
                axis=1,
            ))
        high, low = split(jnp.concatenate(blocks, axis=0))
        green[t] = one_dot(high, spot[...]) + one_dot(low, spot[...])

    for copy in copies[7:12]:
        copy.wait()

    for ch in range(CHUNKS):
        whole(field_out.at[ch], field_in.at[ch], send_sems.at[ch], recv_sems.at[ch]).wait()
        high, low = split(gathered(field_in.at[ch]))
        mixed = one_dot(wide[ch], jnp.concatenate([high, high], axis=0)) + one_dot(
            wide[ch, :, :lines], low
        )
        cosine = jnp.concatenate([twiddle[0]] * 4, axis=0)
        sine = jnp.concatenate([twiddle[1]] * 4, axis=0)
        real, imag = mixed[:lines], mixed[lines:]
        turned = jnp.concatenate(
            [real * cosine + imag * sine, imag * cosine - real * sine], axis=1
        )
        spectrum = dot(split(turned), (inner_t[0], inner_t[1]))
        slots = [
            jnp.where(me == 0, t0, t1) for t0, t1 in zip(slot_lists(0)[ch], slot_lists(1)[ch])
        ]
        kernel_values = jnp.concatenate([green[t] for t in slots], axis=0)
        filtered = spectrum * jnp.concatenate([kernel_values, kernel_values], axis=1)
        back = dot(split(filtered), (inner[0], inner[1]))
        real, imag = back[:, :PLANE], back[:, PLANE:]
        turned = jnp.concatenate(
            [real * cosine - imag * sine, imag * cosine + real * sine], axis=0
        )
        interleaved(dot((gather[ch, 0], gather[ch, 1]), split(turned)), back_out.at[ch])
        send(back_out.at[ch], back_in.at[ch], CHUNKS + ch)

    scale = 1.0 / float(CX * rows * CY * cols * NZ)

    def down(values):
        return jnp.sum(values, axis=0, keepdims=True)

    sums = [[0.0] * 4 for _ in range(atoms // width)]
    for ch in range(CHUNKS):
        index = CHUNKS + ch
        whole(back_out.at[ch], back_in.at[ch], send_sems.at[index], recv_sems.at[index]).wait()
        high, low = split((gathered(back_in.at[ch]) * scale).T[:TOP])
        both = jnp.concatenate([high, low], axis=1)
        mine = slice(ch * lines, (ch + 1) * lines)
        for k in range(atoms // width):
            cut = slice(k * width, (k + 1) * width)
            for which in range(2):
                near = zf[which, 0, mine, cut]
                sampled[which, :, cut] = one_dot(
                    both, jnp.concatenate([near, near], axis=0)
                ) + one_dot(high, zf[which, 1, mine, cut])
            by_y = by_dy = by_yz = 0.0
            for y in range(EXT_Y):
                row = slice(y * CX, (y + 1) * CX)
                weight = y_rows[0, y : y + 1, cut]
                by_y = by_y + weight * sampled[0, row, cut]
                by_dy = by_dy + y_rows[1, y : y + 1, cut] * sampled[0, row, cut]
                by_yz = by_yz + weight * sampled[1, row, cut]
            by_x = by_dx = by_xz = 0.0
            for x in range(3):
                row = slice(base + x * HALO_ROWS, base + (x + 1) * HALO_ROWS)
                weight = x_rows[0, CX + x : CX + x + 1, cut]
                by_x = by_x + weight * sampled[0, row, cut]
                by_dx = by_dx + x_rows[1, CX + x : CX + x + 1, cut] * sampled[0, row, cut]
                by_xz = by_xz + weight * sampled[1, row, cut]
            xs, dxs = x_rows[0, :CX, cut], x_rows[1, :CX, cut]
            ys, dys = y_rows[0, :, cut], y_rows[1, :, cut]
            found = [
                down(xs * by_y) + down(ys * by_x),
                down(dxs * by_y) + down(ys * by_dx),
                down(xs * by_dy) + down(dys * by_x),
                down(xs * by_yz) + down(ys * by_xz),
            ]
            sums[k] = [a + b for a, b in zip(sums[k], found)]
    for k in range(atoms // width):
        cut = slice(k * width, (k + 1) * width)
        part = neutral[:, cut]
        value, grad_x, grad_y, grad_z = sums[k]
        energy_ref[:, cut] = 0.5 * part * value
        forces_ref[0:1, cut] = -part * grad_x
        forces_ref[1:2, cut] = -part * grad_y
        forces_ref[2:3, cut] = -part * grad_z


def fast_body(plan, charges, structure_id, live_count, cell_index, fraction, influence):
    rows, cols, offsets, diffs = plan
    n = rows * cols
    atoms = charges.shape[0]
    tables = make_tables(rows, cols)
    vmem = pl.BlockSpec(memory_space=pltpu.VMEM)
    anywhere = pl.BlockSpec(memory_space=pltpu.HBM)
    f32, bf16 = jnp.float32, jnp.bfloat16
    stored = influence.reshape(2, n, CX, CX * rows)
    inputs = [
        charges[None, :], structure_id[None, :], live_count, cell_index, fraction, stored,
    ]
    held = [
        pltpu.SMEM(v.shape, v.dtype) if v is live_count else pltpu.VMEM(v.shape, v.dtype)
        for v in inputs
    ]
    for i, table in enumerate(tables):
        held.append(pltpu.VMEM(table.shape[1:] if i in (1, 2) else table.shape, table.dtype))
    sems = pltpu.SemaphoreType.DMA
    exchanged = pltpu.VMEM((CHUNKS, n, 8, LANES), f32)
    forces, energy = pl.pallas_call(
        functools.partial(kernel, plan),
        out_shape=(
            jax.ShapeDtypeStruct((3, atoms), f32),
            jax.ShapeDtypeStruct((1, atoms), f32),
        ),
        in_specs=[anywhere] * (len(inputs) + len(tables)),
        out_specs=(vmem, vmem),
        scratch_shapes=held + [
            pltpu.VMEM((2, NZ, atoms), bf16),
            pltpu.VMEM((2, NZ, atoms), bf16),
            pltpu.VMEM((2, 2, NZ, atoms), bf16),
            pltpu.VMEM((2, PLANE, atoms), bf16),
            pltpu.VMEM((2, 16, atoms), f32),
            pltpu.VMEM((2, HALO_ROWS, atoms), f32),
            pltpu.VMEM((len(diffs), S_DEV, LANES), f32),
            pltpu.VMEM((n, 8, LANES), f32),
            pltpu.VMEM((n, 8, LANES), f32),
            pltpu.VMEM((8, n, LANES), f32),
            exchanged, exchanged, exchanged, exchanged,
            pltpu.VMEM((2, TOP, atoms), f32),
            sems((len(held),)),
            sems((len(diffs),)), sems((len(diffs),)), sems(()), sems(()),
            sems((2 * CHUNKS,)), sems((2 * CHUNKS,)),
        ],
        compiler_params=pltpu.CompilerParams(
            collective_id=0, has_side_effects=True, vmem_limit_bytes=67043328
        ),
        name="ewald_step",
    )(*inputs, *[jnp.asarray(t) for t in tables])
    return forces, energy[0]


def solution(mesh):
    plan = make_plan(mesh.shape["row"], mesh.shape["col"])
    placed = (
        P(("row", "col")),
        P(("row", "col")),
        P(("row", "col")),
        P(None, ("row", "col")),
        P(None, ("row", "col")),
        P("col", "row", None),
    )
    return jax.shard_map(
        body if plan is None else functools.partial(fast_body, plan),
        mesh=mesh,
        in_specs=placed,
        out_specs=(P(None, ("row", "col")), P(("row", "col"))),
        check_vma=False,
    )
```

time: 40.1 us -> 32.9 us (0.82)
  Pallas kernels: 33.3 us -> 29.5 us
  local copies, waits for them, and re-layouts: 4.85 us -> 1.92 us
    pallas_call x1, Pallas kernels: 33.3 us -> 29.5 us  [fast_body(): pl.pallas_call(functools.partial(kernel, plan), out_shape=(jax.ShapeDtype...]
    reshape x2 -> x0, local copies, waits for them, and re-layouts: 1.6 us -> none  [the longest x1 1.28 us: fast_body(): stored.transpose(1, 4, 2, 0, 3, 5).reshape(n, CX, high * per_col * n)]
    transpose x1 -> x0, local copies, waits for them, and re-layouts: 0.87 us -> none  [fast_body(): stored.transpose(1, 4, 2, 0, 3, 5).reshape(n, CX, high * per_col * n)]
    unnamed x21 -> x4, local copies, waits for them, and re-layouts: 2.39 us -> 1.92 us
where the time goes in v1:
time: 32.9 us; the launch traced here: 32.7 us
  Pallas kernels  29.5 us (90%)
  local copies, waits for them, and re-layouts  1.92 us (6%)
  between operations  1.29 us (4%)
    pallas_call x1, Pallas kernels, fast_body(): pl.pallas_call(functools.partial(kernel, plan), out_shape=(jax.ShapeDtype...  29.5 us
    unnamed x4, local copies, waits for them, and re-layouts  1.92 us

profile of v1, /device:TPU:0, one launch (start us, length us, event | category | flops | bytes accessed | tf_op | source)
XLA Modules:
  0.0 32.7 jit_solution(7700258642312506058)
XLA Ops:
  1.3 29.5 %ewald_step.1 = (f32[3,1024]{1,0:T(4,128)}, f32[1,1024]{1,0:T(1,128)}) custom-call(f32[1,1024]{1,0:T(1,128)} %bitcast.5, s32[1,1024]{1,0:T(1,128)} %bitcast.6, s32[1]{0:T(128)S(6)} %copy.17.live_hbm, s32[3,1024]{1,0:T(4,128)} %cell_hbm.1, f32[3,1024]{1,0:T(4,128)} %frac_hbm.1, f32[2,32,8,64]{3,2,1,0:T(8,128)} %bitcast.4, ...), custom_call_target="tpu_custom_call" | custom-call | tf_op jit(solution)/shard_map/ewald_step/pallas_call | solution.py:661
  30.8 0.0 copy-start
  30.8 1.3 %copy.18 = f32[3,1024]{1,0:T(4,128)} copy(f32[3,1024]{1,0:T(4,128)} %get-tuple-element.8) | data formatting | bytes 24576
  32.1 0.0 copy-done
  32.1 0.6 %copy.19 = f32[1024]{0:T(1024)} copy(f32[1024]{0:T(1024)S(1)} %bitcast.7) | data formatting | bytes 8192
Async XLA Ops:
  30.8 1.3 %copy-start = (f32[1,1024]{1,0:T(1,128)S(1)}, f32[1,1024]{1,0:T(1,128)}, u32[]{:S(2)}) copy-start(f32[1,1024]{1,0:T(1,128)} %get-tuple-element.5) | copy-start | bytes 12292

commit v2 on v1

--- a/solution.py
+++ b/solution.py
@@ -310,6 +310,12 @@
     )
 
 
+def tall_dot(left, right, contract=(1, 0)):
+    height = left[0].shape[0]
+    stacked = one_dot(jnp.concatenate(left, axis=0), right[0], contract)
+    return stacked[:height] + (stacked[height:] + one_dot(left[0], right[1], contract))
+
+
 def pick(distance, weights):
     result = jnp.where(distance == 3, weights[3], 0.0)
     for i in (2, 1, 0):
@@ -325,7 +331,7 @@
     charges_ref, sid_ref, live_ref, cell_ref, frac_ref, raw,
     fz, wide, gather, twiddle, inner_t, inner, spot,
     z_rows, z_slopes, zf, plane, x_rows, y_rows,
-    frag, inf_out, inf_in, green,
+    member, frag_out, frag_in, inf_out, inf_in, green,
     field_out, field_in, back_out, back_in, sampled,
     local_sems, frag_send, frag_recv, inf_send, inf_recv, send_sems, recv_sems,
 ):
@@ -336,10 +342,13 @@
     atoms = charges_ref.shape[1]
     lines = NZ // CHUNKS
     kind = jnp.minimum(me, 1)
-    far_first = sorted(range(1, n), key=lambda o: -o)
+    far_first = sorted(range(1, n), key=lambda o: o)
+
+    def other(o):
+        return lax.rem(me + o, n)
 
     def peer(o):
-        return (r ^ (o // cols), c ^ (o % cols))
+        return (lax.div(other(o), cols), lax.rem(other(o), cols))
 
     barrier = pltpu.get_barrier_semaphore()
     for o in far_first:
@@ -374,26 +383,47 @@
     charged = charges * live
     sid = sid_ref[...]
     within = lax.broadcasted_iota(jnp.int32, (S_DEV, atoms), 0)
-    owners = [
-        lax.rem(r + a % rows, rows) * cols + lax.rem(c + b % cols, cols) for a, b in offsets
+    count = len(offsets)
+    held = [
+        sid == within + S_DEV * (
+            lax.rem(r + a % rows, rows) * cols + lax.rem(c + b % cols, cols)
+        )
+        for a, b in offsets
     ]
-
-    def belongs(o):
-        return sid == within + owners[o] * S_DEV
-
-    def folded(values):
-        total = values[:, :LANES]
-        for k in range(1, atoms // LANES):
-            total = total + values[:, k * LANES : (k + 1) * LANES]
-        return jnp.sum(total, axis=1, keepdims=True)
-
-    tile_lane = lax.broadcasted_iota(jnp.int32, (S_DEV, LANES), 1)
-    message = jnp.zeros((S_DEV, LANES), jnp.float32)
-    for o in range(len(offsets)):
-        mine = belongs(o)
-        message = jnp.where(tile_lane == 2 * o, folded(jnp.where(mine, charged, 0.0)), message)
-        message = jnp.where(tile_lane == 2 * o + 1, folded(jnp.where(mine, live, 0.0)), message)
-    frag[0] = message
+    for i in range(0, count, 2):
+        chosen = jnp.concatenate([jnp.where(h, 1.0, 0.0) for h in held[i : i + 2]], axis=0)
+        member[i * S_DEV : (i + 2) * S_DEV, :] = chosen.astype(jnp.bfloat16)
+    member[count * S_DEV :, :] = jnp.zeros((LANES - count * S_DEV, atoms), jnp.bfloat16)
+
+    def thirds(values):
+        first = values.astype(jnp.bfloat16).astype(jnp.float32)
+        second = (values - first).astype(jnp.bfloat16).astype(jnp.float32)
+        return [first, second, values - first - second]
+
+    weighed = thirds(charged) + [live, jnp.zeros((12, atoms), jnp.float32)]
+    weighed = jnp.concatenate(weighed, axis=0).astype(jnp.bfloat16)
+    local_sums = one_dot(weighed, member[...], (1, 1))
+    local_sums = jnp.concatenate(
+        [
+            local_sums[0:1] + local_sums[1:2] + local_sums[2:3],
+            local_sums[3:4],
+            jnp.zeros((6, LANES), jnp.float32),
+        ],
+        axis=0,
+    )
+    tile_lane = lax.broadcasted_iota(jnp.int32, (8, LANES), 1)
+    shifted = {
+        k: local_sums if k == 0 else pltpu.roll(local_sums, S_DEV * k % LANES, 1)
+        for k in range(1 - count, count)
+    }
+    messages = [jnp.zeros((8, LANES), jnp.float32) for _ in diffs]
+    for j, (a, b) in enumerate(offsets):
+        for i, (d, e) in enumerate(offsets):
+            k = diffs.index(((a - d) % rows, (b - e) % cols))
+            messages[k] = jnp.where(tile_lane // S_DEV == j, shifted[j - i], messages[k])
+    frag_in[0] = messages[0][:2]
+    for k in range(1, len(diffs)):
+        frag_out[k] = messages[k][:2]
 
     for copy in copies[3:5]:
         copy.wait()
@@ -422,9 +452,6 @@
             zf[which, 0, :, cut], zf[which, 1, :, cut] = split(value)
 
     fill(z_rows, wz)
-    copies[6].wait()
-    transform(0, z_rows)
-
     copies[5].wait()
     for p in range(n):
         first, second = raw[0, p], raw[1, p]
@@ -438,7 +465,7 @@
         a, b = diffs[k]
         target = (lax.rem(r + (-a) % rows, rows), lax.rem(c + (-b) % cols, cols))
         return pltpu.make_async_remote_copy(
-            frag.at[0], frag.at[k], frag_send.at[k], frag_recv.at[k],
+            frag_out.at[k], frag_in.at[k], frag_send.at[k], frag_recv.at[k],
             device_id=target, device_id_type=MESH,
         )
 
@@ -453,11 +480,13 @@
 
     for o in far_first:
         pltpu.make_async_remote_copy(
-            inf_out.at[residue(me ^ o)], inf_in.at[place], inf_send, inf_recv,
+            inf_out.at[residue(other(o))], inf_in.at[place], inf_send, inf_recv,
             device_id=peer(o), device_id_type=MESH,
         ).start()
     inf_in[place] = inf_out[residue(me)]
 
+    copies[6].wait()
+    transform(0, z_rows)
     fill(z_slopes, vz)
     transform(1, z_slopes)
     distance = lax.broadcasted_iota(jnp.int32, (16, atoms), 0) - (cell_ref[0:1, :] - r * CX)
@@ -472,18 +501,13 @@
 
     for copy in frags:
         copy.wait()
-    slot = {diff: k for k, diff in enumerate(diffs)}
-    mean = jnp.zeros((S_DEV, atoms), jnp.float32)
-    for j, (a, b) in enumerate(offsets):
-        total = jnp.zeros((S_DEV, LANES), jnp.float32)
-        for i, (d, e) in enumerate(offsets):
-            part = frag[slot[((a - d) % rows, (b - e) % cols)]]
-            total = total + jnp.where(tile_lane // 2 == i, part, 0.0)
-        odd = tile_lane % 2 == 1
-        charge_sum = jnp.sum(jnp.where(odd, 0.0, total), axis=1, keepdims=True)
-        live_sum = jnp.sum(jnp.where(odd, total, 0.0), axis=1, keepdims=True)
-        mean = jnp.where(belongs(j), charge_sum / live_sum, mean)
-    mean = jnp.sum(mean, axis=0, keepdims=True)
+    total = frag_in[0]
+    for k in range(1, len(diffs)):
+        total = total + frag_in[k]
+    mean = jnp.where(tile_lane[:1] < count * S_DEV, total[0:1] / total[1:2], 0.0)
+    mean = jnp.concatenate(thirds(mean) + [jnp.zeros((13, LANES), jnp.float32)], axis=0)
+    mean = one_dot(mean.astype(jnp.bfloat16), member[...])
+    mean = mean[0:1] + mean[1:2] + mean[2:3]
     neutral = (charges - mean) * live
 
     x_charged = x_rows[0, :CX] * neutral
@@ -522,7 +546,7 @@
     def send(source, target, index):
         for o in far_first:
             pltpu.make_async_remote_copy(
-                source.at[me ^ o], target.at[me], send_sems.at[index], recv_sems.at[index],
+                source.at[other(o)], target.at[me], send_sems.at[index], recv_sems.at[index],
                 device_id=peer(o), device_id_type=MESH,
             ).start()
         target[me] = source[me]
@@ -535,7 +559,7 @@
 
     for ch in range(CHUNKS):
         mine = slice(ch * lines, (ch + 1) * lines)
-        value = dot((zf[0, 0, mine], zf[0, 1, mine]), (plane[0], plane[1]), (1, 1))
+        value = tall_dot((zf[0, 0, mine], zf[0, 1, mine]), (plane[0], plane[1]), (1, 1))
         interleaved(value, field_out.at[ch])
         send(field_out.at[ch], field_in.at[ch], ch)
 
@@ -572,18 +596,18 @@
         turned = jnp.concatenate(
             [real * cosine + imag * sine, imag * cosine - real * sine], axis=1
         )
-        spectrum = dot(split(turned), (inner_t[0], inner_t[1]))
+        spectrum = tall_dot(split(turned), (inner_t[0], inner_t[1]))
         slots = [
             jnp.where(me == 0, t0, t1) for t0, t1 in zip(slot_lists(0)[ch], slot_lists(1)[ch])
         ]
         kernel_values = jnp.concatenate([green[t] for t in slots], axis=0)
         filtered = spectrum * jnp.concatenate([kernel_values, kernel_values], axis=1)
-        back = dot(split(filtered), (inner[0], inner[1]))
+        back = tall_dot(split(filtered), (inner[0], inner[1]))
         real, imag = back[:, :PLANE], back[:, PLANE:]
         turned = jnp.concatenate(
             [real * cosine - imag * sine, imag * cosine + real * sine], axis=0
         )
-        interleaved(dot((gather[ch, 0], gather[ch, 1]), split(turned)), back_out.at[ch])
+        interleaved(tall_dot((gather[ch, 0], gather[ch, 1]), split(turned)), back_out.at[ch])
         send(back_out.at[ch], back_in.at[ch], CHUNKS + ch)
 
     scale = 1.0 / float(CX * rows * CY * cols * NZ)
@@ -638,6 +662,17 @@
         forces_ref[2:3, cut] = -part * grad_z
 
 
+def put(forces_ref, energy_ref, forces_out, energy_out, sems):
+    copies = [
+        pltpu.make_async_copy(forces_ref, forces_out, sems.at[0]),
+        pltpu.make_async_copy(energy_ref, energy_out, sems.at[1]),
+    ]
+    for copy in copies:
+        copy.start()
+    for copy in copies:
+        copy.wait()
+
+
 def fast_body(plan, charges, structure_id, live_count, cell_index, fraction, influence):
     rows, cols, offsets, diffs = plan
     n = rows * cols
@@ -661,8 +696,8 @@
     forces, energy = pl.pallas_call(
         functools.partial(kernel, plan),
         out_shape=(
-            jax.ShapeDtypeStruct((3, atoms), f32),
-            jax.ShapeDtypeStruct((1, atoms), f32),
+            pltpu.VMEM((3, atoms), f32),
+            pltpu.VMEM((1, atoms), f32),
         ),
         in_specs=[anywhere] * (len(inputs) + len(tables)),
         out_specs=(vmem, vmem),
@@ -673,7 +708,9 @@
             pltpu.VMEM((2, PLANE, atoms), bf16),
             pltpu.VMEM((2, 16, atoms), f32),
             pltpu.VMEM((2, HALO_ROWS, atoms), f32),
-            pltpu.VMEM((len(diffs), S_DEV, LANES), f32),
+            pltpu.VMEM((LANES, atoms), bf16),
+            pltpu.VMEM((len(diffs), 2, LANES), f32),
+            pltpu.VMEM((len(diffs), 2, LANES), f32),
             pltpu.VMEM((n, 8, LANES), f32),
             pltpu.VMEM((n, 8, LANES), f32),
             pltpu.VMEM((8, n, LANES), f32),
@@ -684,10 +721,22 @@
             sems((2 * CHUNKS,)), sems((2 * CHUNKS,)),
         ],
         compiler_params=pltpu.CompilerParams(
-            collective_id=0, has_side_effects=True, vmem_limit_bytes=67043328
+            collective_id=0, has_side_effects=True, vmem_limit_bytes=66000000
         ),
         name="ewald_step",
     )(*inputs, *[jnp.asarray(t) for t in tables])
+    forces, energy = pl.pallas_call(
+        put,
+        out_shape=(
+            jax.ShapeDtypeStruct((3, atoms), f32),
+            jax.ShapeDtypeStruct((1, atoms), f32),
+        ),
+        in_specs=[vmem] * 2,
+        out_specs=(anywhere, anywhere),
+        scratch_shapes=[sems((2,))],
+        compiler_params=pltpu.CompilerParams(vmem_limit_bytes=262144),
+        name="put_results",
+    )(forces, energy)
     return forces, energy[0]
 
 

time: 32.9 us -> 29.1 us (0.88)
  local copies, waits for them, and re-layouts: 1.92 us -> 0 us
  Pallas kernels: 29.5 us -> 27.6 us
    unnamed x4 -> x0, local copies, waits for them, and re-layouts: 1.92 us -> none
    pallas_call x1 -> x2, Pallas kernels: 29.5 us -> 27.6 us  [the longest x1 27 us: fast_body(): pl.pallas_call(functools.partial(kernel, plan), out_shape=(pltpu.VMEM((3,...]
where the time goes in v2:
time: 29.1 us; the launch traced here: 28.9 us
  Pallas kernels  27.6 us (95%)
  between operations  1.28 us (4%)
    pallas_call x1, Pallas kernels, fast_body(): pl.pallas_call(functools.partial(kernel, plan), out_shape=(pltpu.VMEM((3,...  27 us
    pallas_call x1, Pallas kernels, fast_body(): pl.pallas_call(put, out_shape=(jax.ShapeDtypeStruct((3, atoms), f32), jax...  0.63 us

profile of v2, /device:TPU:0, one launch (start us, length us, event | category | flops | bytes accessed | tf_op | source)
XLA Modules:
  0.0 28.9 jit_solution(5987875383957481850)
XLA Ops:
  1.3 27.0 %ewald_step.1 = (f32[3,1024]{1,0:T(4,128)S(1)}, f32[1,1024]{1,0:T(1,128)S(1)}) custom-call(f32[1,1024]{1,0:T(1,128)} %bitcast.5, s32[1,1024]{1,0:T(1,128)} %bitcast.6, s32[1]{0:T(128)S(6)} %copy.15.live_hbm, s32[3,1024]{1,0:T(4,128)} %cell_hbm.1, f32[3,1024]{1,0:T(4,128)} %frac_hbm.1, f32[2,32,8,64]{3,2,1,0:T(8,128)} %bitcast.4, ...), custom_call_target="tpu_custom_call" | custom-call | tf_op jit(solution)/shard_map/ewald_step/pallas_call | solution.py:696
  28.3 0.6 %put_results.1 = (f32[3,1024]{1,0:T(4,128)}, f32[1,1024]{1,0:T(1,128)}) custom-call(f32[3,1024]{1,0:T(4,128)S(1)} %get-tuple-element.6.forces_ref, f32[1,1024]{1,0:T(1,128)S(1)} %get-tuple-element.7.energy_ref), custom_call_target="tpu_custom_call" | custom-call | tf_op jit(solution)/shard_map/put_results/pallas_call | solution.py:728

commit v3 on v2

--- a/solution.py
+++ b/solution.py
@@ -161,7 +161,7 @@
 PLANE = 256
 LANES = 128
 TOP = EXT_Y * CX + 3 * HALO_ROWS
-CHUNKS = 2
+CHUNKS = 4
 MESH = pl.DeviceIdType.MESH
 
 
@@ -209,8 +209,8 @@
 
 def slot_lists(kind):
     if kind:
-        return ((0, 1, 6, 7), (2, 3, 4, 5))
-    return ((0, 1, 4, 7), (2, 3, 5, 6))
+        return ((0, 7), (1, 6), (2, 5), (3, 4))
+    return ((0, 4), (1, 7), (2, 6), (3, 5))
 
 
 def make_tables(rows, cols):
@@ -256,7 +256,7 @@
             js = slice(ch * per_chunk, (ch + 1) * per_chunk)
             chunked[kind, ch] = gather[kind][:, :, js][:, :, :, :, list(slot_lists(kind)[ch])]
     lines = 2 * per_chunk * n
-    gather = chunked.reshape(2, CHUNKS, lines, slots * n)
+    gather = chunked.reshape(2, CHUNKS, lines, 2 * slots // CHUNKS * n)
 
     cells, used = plane_cells()
     x, y = cells[:, 0], cells[:, 1]
@@ -280,12 +280,14 @@
         low = (table - high.astype(np.float32)).astype(jnp.bfloat16)
         return np.stack([high, low], axis=axis)
 
-    turned = gather.transpose(0, 1, 3, 2)
-    wide = np.concatenate(list(pair(turned, 0)), axis=-1)
+    def tripled(table):
+        high, low = pair(table, 0)
+        return np.concatenate([high, low, high], axis=-1)
+
     return (
         pair(forward_z, 0),
-        wide,
-        pair(gather, 2),
+        tripled(gather.transpose(0, 1, 3, 2)),
+        tripled(gather),
         twiddle.astype(np.float32),
         pair(inner.T, 0),
         pair(inner, 0),
@@ -314,6 +316,11 @@
     height = left[0].shape[0]
     stacked = one_dot(jnp.concatenate(left, axis=0), right[0], contract)
     return stacked[:height] + (stacked[height:] + one_dot(left[0], right[1], contract))
+
+
+def tripled_rows(values):
+    high, low = split(values)
+    return jnp.concatenate([high, high, low], axis=0)
 
 
 def pick(distance, weights):
@@ -332,7 +339,8 @@
     fz, wide, gather, twiddle, inner_t, inner, spot,
     z_rows, z_slopes, zf, plane, x_rows, y_rows,
     member, frag_out, frag_in, inf_out, inf_in, green,
-    field_out, field_in, back_out, back_in, sampled,
+    field_out, field_in, field_end, field_end_in, back_out, back_in, back_end, back_end_in,
+    spare, sampled,
     local_sems, frag_send, frag_recv, inf_send, inf_recv, send_sems, recv_sems,
 ):
     rows, cols, offsets, diffs = plan
@@ -524,24 +532,14 @@
     tail = jnp.concatenate(tail, axis=0)
     plane[0, base - CX : TOP, :], plane[1, base - CX : TOP, :] = split(tail)
 
-    sub_low = lax.broadcasted_iota(jnp.int32, (8, LANES), 0) < 4
-
-    def interleaved(values, target):
-        for v in range(n // 2):
-            rows8 = slice(8 * v, 8 * v + 8)
-            near, far = values[rows8, :LANES], values[rows8, LANES:]
-            target[2 * v] = jnp.where(sub_low, near, pltpu.roll(far, 4, 0))
-            target[2 * v + 1] = jnp.where(sub_low, pltpu.roll(near, 4, 0), far)
+    per = lines // n
+
+    def spread_out(values, target):
+        for p in range(n):
+            target[p] = values[per * p : per * (p + 1)]
 
     def gathered(source):
-        near, far = [], []
-        for v in range(n // 2):
-            first, second = source[2 * v], source[2 * v + 1]
-            near.append(jnp.where(sub_low, first, pltpu.roll(second, 4, 0)))
-            far.append(jnp.where(sub_low, pltpu.roll(first, 4, 0), second))
-        return jnp.concatenate(
-            [jnp.concatenate(near, axis=0), jnp.concatenate(far, axis=0)], axis=1
-        )
+        return jnp.concatenate([source[p] for p in range(n)], axis=0)
 
     def send(source, target, index):
         for o in far_first:
@@ -557,11 +555,46 @@
             device_id=(r, c), device_id_type=MESH,
         )
 
-    for ch in range(CHUNKS):
-        mine = slice(ch * lines, (ch + 1) * lines)
-        value = tall_dot((zf[0, 0, mine], zf[0, 1, mine]), (plane[0], plane[1]), (1, 1))
-        interleaved(value, field_out.at[ch])
+    part_lane = lax.broadcasted_iota(jnp.int32, (lines, LANES), 1)
+    third = PLANE - TOP
+
+    def lent(values, extra, k):
+        tail = values[:, LANES:]
+        moved = pltpu.roll(extra, LANES - third * (k + 1), 1)
+        return jnp.concatenate(
+            [values[:, :LANES], jnp.where(part_lane < LANES - third, tail, moved)], axis=1
+        )
+
+    def returned(tails):
+        result = pltpu.roll(tails[-1], third * CHUNKS - third, 1)
+        for k in range(CHUNKS - 2, -1, -1):
+            result = jnp.where(
+                part_lane < third * (k + 1), pltpu.roll(tails[k], third * (k + 1), 1), result
+            )
+        return result
+
+    last = CHUNKS - 1
+
+    def field_of(chunks):
+        rows_of = [
+            jnp.concatenate(
+                [zf[0, half, ch * lines : (ch + 1) * lines, :] for ch in chunks], axis=0
+            )
+            for half in range(2)
+        ]
+        value = tall_dot(rows_of, (plane[0], plane[1]), (1, 1))
+        return [value[i * lines : (i + 1) * lines] for i in range(len(chunks))]
+
+    first, end = field_of([0, last])
+    end_tail = end[:, LANES:]
+    spread_out(lent(first, end_tail, 0), field_out.at[0])
+    send(field_out.at[0], field_in.at[0], 0)
+    middle = field_of(list(range(1, last)))
+    for ch in range(1, last):
+        spread_out(lent(middle[ch - 1], end_tail, ch), field_out.at[ch])
         send(field_out.at[ch], field_in.at[ch], ch)
+    spread_out(end[:, :LANES], field_end)
+    send(field_end, field_end_in, last)
 
     whole(inf_out, inf_in, inf_send, inf_recv).wait()
     copies[12].wait()
@@ -585,13 +618,17 @@
         copy.wait()
 
     for ch in range(CHUNKS):
-        whole(field_out.at[ch], field_in.at[ch], send_sems.at[ch], recv_sems.at[ch]).wait()
-        high, low = split(gathered(field_in.at[ch]))
-        mixed = one_dot(wide[ch], jnp.concatenate([high, high], axis=0)) + one_dot(
-            wide[ch, :, :lines], low
-        )
-        cosine = jnp.concatenate([twiddle[0]] * 4, axis=0)
-        sine = jnp.concatenate([twiddle[1]] * 4, axis=0)
+        if ch < last:
+            whole(field_out.at[ch], field_in.at[ch], send_sems.at[ch], recv_sems.at[ch]).wait()
+            arrived = gathered(field_in.at[ch])
+        else:
+            whole(field_end, field_end_in, send_sems.at[ch], recv_sems.at[ch]).wait()
+            tails = [gathered(field_in.at[k])[:, LANES:] for k in range(last)]
+            arrived = jnp.concatenate([gathered(field_end_in), returned(tails)], axis=1)
+        mixed = one_dot(wide[ch], tripled_rows(arrived))
+        repeats = lines // n
+        cosine = jnp.concatenate([twiddle[0]] * repeats, axis=0)
+        sine = jnp.concatenate([twiddle[1]] * repeats, axis=0)
         real, imag = mixed[:lines], mixed[lines:]
         turned = jnp.concatenate(
             [real * cosine + imag * sine, imag * cosine - real * sine], axis=1
@@ -607,28 +644,57 @@
         turned = jnp.concatenate(
             [real * cosine - imag * sine, imag * cosine + real * sine], axis=0
         )
-        interleaved(tall_dot((gather[ch, 0], gather[ch, 1]), split(turned)), back_out.at[ch])
-        send(back_out.at[ch], back_in.at[ch], CHUNKS + ch)
+        value = one_dot(gather[ch], tripled_rows(turned))
+        if ch == 0:
+            spare[...] = value[:, LANES:]
+            spread_out(value[:, :LANES], back_end)
+            send(back_end, back_end_in, CHUNKS)
+        else:
+            spread_out(lent(value, spare[...], ch - 1), back_out.at[ch - 1])
+            send(back_out.at[ch - 1], back_in.at[ch - 1], CHUNKS + ch)
 
     scale = 1.0 / float(CX * rows * CY * cols * NZ)
 
     def down(values):
         return jnp.sum(values, axis=0, keepdims=True)
 
+    def turned_rows(values):
+        found = (values * scale).T
+        high = found.astype(jnp.bfloat16).astype(jnp.float32)
+        return jnp.concatenate([high, found - high, high], axis=1).astype(jnp.bfloat16)
+
+    inside, outside = {}, {}
     sums = [[0.0] * 4 for _ in range(atoms // width)]
-    for ch in range(CHUNKS):
+    for ch in range(1, CHUNKS):
+        if ch == 1:
+            whole(back_end, back_end_in, send_sems.at[CHUNKS], recv_sems.at[CHUNKS]).wait()
+            inside[0] = turned_rows(gathered(back_end_in))
         index = CHUNKS + ch
-        whole(back_out.at[ch], back_in.at[ch], send_sems.at[index], recv_sems.at[index]).wait()
-        high, low = split((gathered(back_in.at[ch]) * scale).T[:TOP])
-        both = jnp.concatenate([high, low], axis=1)
-        mine = slice(ch * lines, (ch + 1) * lines)
+        whole(
+            back_out.at[ch - 1], back_in.at[ch - 1], send_sems.at[index], recv_sems.at[index]
+        ).wait()
+        arrived = gathered(back_in.at[ch - 1])
+        both = turned_rows(arrived)
+        inside[ch], outside[ch] = both[:LANES], both[LANES:TOP]
+        if ch == last:
+            tails = [gathered(back_in.at[k])[:, LANES:] for k in range(last)]
+            outside[0] = turned_rows(returned(tails))[: TOP - LANES]
         for k in range(atoms // width):
             cut = slice(k * width, (k + 1) * width)
             for which in range(2):
-                near = zf[which, 0, mine, cut]
-                sampled[which, :, cut] = one_dot(
-                    both, jnp.concatenate([near, near], axis=0)
-                ) + one_dot(high, zf[which, 1, mine, cut])
+                def stacked(c):
+                    near = zf[which, 0, c * lines : (c + 1) * lines, cut]
+                    far = zf[which, 1, c * lines : (c + 1) * lines, cut]
+                    return jnp.concatenate([near, near, far], axis=0)
+
+                here = one_dot(inside[ch], stacked(ch))
+                if ch == 1:
+                    here = here + one_dot(inside[0], stacked(0))
+                there = one_dot(outside[ch], stacked(ch))
+                if ch == last:
+                    there = there + one_dot(outside[0], stacked(0))
+                sampled[which, :LANES, cut] = here
+                sampled[which, LANES:, cut] = there
             by_y = by_dy = by_yz = 0.0
             for y in range(EXT_Y):
                 row = slice(y * CX, (y + 1) * CX)
@@ -692,7 +758,8 @@
     for i, table in enumerate(tables):
         held.append(pltpu.VMEM(table.shape[1:] if i in (1, 2) else table.shape, table.dtype))
     sems = pltpu.SemaphoreType.DMA
-    exchanged = pltpu.VMEM((CHUNKS, n, 8, LANES), f32)
+    exchanged = pltpu.VMEM((CHUNKS - 1, n, NZ // CHUNKS // n, PLANE), f32)
+    short = pltpu.VMEM((n, NZ // CHUNKS // n, LANES), f32)
     forces, energy = pl.pallas_call(
         functools.partial(kernel, plan),
         out_shape=(
@@ -714,7 +781,8 @@
             pltpu.VMEM((n, 8, LANES), f32),
             pltpu.VMEM((n, 8, LANES), f32),
             pltpu.VMEM((8, n, LANES), f32),
-            exchanged, exchanged, exchanged, exchanged,
+            exchanged, exchanged, short, short, exchanged, exchanged, short, short,
+            pltpu.VMEM((NZ // CHUNKS, LANES), f32),
             pltpu.VMEM((2, TOP, atoms), f32),
             sems((len(held),)),
             sems((len(diffs),)), sems((len(diffs),)), sems(()), sems(()),

time: 29.1 us -> 28.8 us (0.990)
  Pallas kernels: 27.6 us -> 27.3 us
where the time goes in v3:
time: 28.8 us; the launch traced here: 28.6 us
  Pallas kernels  27.3 us (95%)
  between operations  1.28 us (4%)
    pallas_call x1, Pallas kernels, fast_body(): pl.pallas_call(functools.partial(kernel, plan), out_shape=(pltpu.VMEM((3,...  26.7 us
    pallas_call x1, Pallas kernels, fast_body(): pl.pallas_call(put, out_shape=(jax.ShapeDtypeStruct((3, atoms), f32), jax...  0.63 us

profile of v3, /device:TPU:0, one launch (start us, length us, event | category | flops | bytes accessed | tf_op | source)
XLA Modules:
  0.0 28.6 jit_solution(4541292777018058397)
XLA Ops:
  1.3 26.7 %ewald_step.1 = (f32[3,1024]{1,0:T(4,128)S(1)}, f32[1,1024]{1,0:T(1,128)S(1)}) custom-call(f32[1,1024]{1,0:T(1,128)} %bitcast.5, s32[1,1024]{1,0:T(1,128)} %bitcast.6, s32[1]{0:T(128)S(6)} %copy.15.live_hbm, s32[3,1024]{1,0:T(4,128)} %cell_hbm.1, f32[3,1024]{1,0:T(4,128)} %frac_hbm.1, f32[2,32,8,64]{3,2,1,0:T(8,128)} %bitcast.4, ...), custom_call_target="tpu_custom_call" | custom-call | tf_op jit(solution)/shard_map/ewald_step/pallas_call | solution.py:763
  28.0 0.6 %put_results.1 = (f32[3,1024]{1,0:T(4,128)}, f32[1,1024]{1,0:T(1,128)}) custom-call(f32[3,1024]{1,0:T(4,128)S(1)} %get-tuple-element.6.forces_ref, f32[1,1024]{1,0:T(1,128)S(1)} %get-tuple-element.7.energy_ref), custom_call_target="tpu_custom_call" | custom-call | tf_op jit(solution)/shard_map/put_results/pallas_call | solution.py:796

commit v4 on v3

--- a/solution.py
+++ b/solution.py
@@ -495,8 +495,6 @@
 
     copies[6].wait()
     transform(0, z_rows)
-    fill(z_slopes, vz)
-    transform(1, z_slopes)
     distance = lax.broadcasted_iota(jnp.int32, (16, atoms), 0) - (cell_ref[0:1, :] - r * CX)
     x_rows[0] = pick(distance, wx)
     x_rows[1] = pick(distance, vx)
@@ -596,6 +594,8 @@
     spread_out(end[:, :LANES], field_end)
     send(field_end, field_end_in, last)
 
+    fill(z_slopes, vz)
+    transform(1, z_slopes)
     whole(inf_out, inf_in, inf_send, inf_recv).wait()
     copies[12].wait()
     group = lax.broadcasted_iota(jnp.int32, (8, LANES), 1) % rows
@@ -663,22 +663,22 @@
         high = found.astype(jnp.bfloat16).astype(jnp.float32)
         return jnp.concatenate([high, found - high, high], axis=1).astype(jnp.bfloat16)
 
-    inside, outside = {}, {}
     sums = [[0.0] * 4 for _ in range(atoms // width)]
     for ch in range(1, CHUNKS):
+        piece = None
         if ch == 1:
             whole(back_end, back_end_in, send_sems.at[CHUNKS], recv_sems.at[CHUNKS]).wait()
-            inside[0] = turned_rows(gathered(back_end_in))
+            piece = turned_rows(gathered(back_end_in))
+            piece_rows = slice(0, LANES)
         index = CHUNKS + ch
         whole(
             back_out.at[ch - 1], back_in.at[ch - 1], send_sems.at[index], recv_sems.at[index]
         ).wait()
-        arrived = gathered(back_in.at[ch - 1])
-        both = turned_rows(arrived)
-        inside[ch], outside[ch] = both[:LANES], both[LANES:TOP]
+        full = turned_rows(gathered(back_in.at[ch - 1]))[:TOP]
         if ch == last:
             tails = [gathered(back_in.at[k])[:, LANES:] for k in range(last)]
-            outside[0] = turned_rows(returned(tails))[: TOP - LANES]
+            piece = turned_rows(returned(tails))[: TOP - LANES]
+            piece_rows = slice(LANES, TOP)
         for k in range(atoms // width):
             cut = slice(k * width, (k + 1) * width)
             for which in range(2):
@@ -687,14 +687,14 @@
                     far = zf[which, 1, c * lines : (c + 1) * lines, cut]
                     return jnp.concatenate([near, near, far], axis=0)
 
-                here = one_dot(inside[ch], stacked(ch))
-                if ch == 1:
-                    here = here + one_dot(inside[0], stacked(0))
-                there = one_dot(outside[ch], stacked(ch))
-                if ch == last:
-                    there = there + one_dot(outside[0], stacked(0))
-                sampled[which, :LANES, cut] = here
-                sampled[which, LANES:, cut] = there
+                most = one_dot(full, stacked(ch))
+                if piece is None:
+                    sampled[which, :, cut] = most
+                    continue
+                more = one_dot(piece, stacked(0))
+                for part in (slice(0, LANES), slice(LANES, TOP)):
+                    value = most[part]
+                    sampled[which, part, cut] = value + more if part == piece_rows else value
             by_y = by_dy = by_yz = 0.0
             for y in range(EXT_Y):
                 row = slice(y * CX, (y + 1) * CX)

time: 28.8 us -> 28.8 us (level)
  no operation moved by 1% of the time
where the time goes in v4:
time: 28.8 us; the launch traced here: 28.6 us
  Pallas kernels  27.3 us (95%)
  between operations  1.28 us (4%)
    pallas_call x1, Pallas kernels, fast_body(): pl.pallas_call(functools.partial(kernel, plan), out_shape=(pltpu.VMEM((3,...  26.7 us
    pallas_call x1, Pallas kernels, fast_body(): pl.pallas_call(put, out_shape=(jax.ShapeDtypeStruct((3, atoms), f32), jax...  0.63 us

profile of v4, /device:TPU:0, one launch (start us, length us, event | category | flops | bytes accessed | tf_op | source)
XLA Modules:
  0.0 28.6 jit_solution(15965299542846732025)
XLA Ops:
  1.3 26.7 %ewald_step.1 = (f32[3,1024]{1,0:T(4,128)S(1)}, f32[1,1024]{1,0:T(1,128)S(1)}) custom-call(f32[1,1024]{1,0:T(1,128)} %bitcast.5, s32[1,1024]{1,0:T(1,128)} %bitcast.6, s32[1]{0:T(128)S(6)} %copy.15.live_hbm, s32[3,1024]{1,0:T(4,128)} %cell_hbm.1, f32[3,1024]{1,0:T(4,128)} %frac_hbm.1, f32[2,32,8,64]{3,2,1,0:T(8,128)} %bitcast.4, ...), custom_call_target="tpu_custom_call" | custom-call | tf_op jit(solution)/shard_map/ewald_step/pallas_call | solution.py:763
  28.0 0.6 %put_results.1 = (f32[3,1024]{1,0:T(4,128)}, f32[1,1024]{1,0:T(1,128)}) custom-call(f32[3,1024]{1,0:T(4,128)S(1)} %get-tuple-element.6.forces_ref, f32[1,1024]{1,0:T(1,128)S(1)} %get-tuple-element.7.energy_ref), custom_call_target="tpu_custom_call" | custom-call | tf_op jit(solution)/shard_map/put_results/pallas_call | solution.py:796
